TPU v7x, 256 devices: a whole 4x4x8 slice. The times are simulated.
256 devices in a mesh: dp: 32 (over z, x_hi, core), expert: 8 (over x_lo, y).
Axes of the slice: x: 4 (x_hi: 2, x_lo: 2; x = x_hi * 2 + x_lo), y: 4, z: 8, core: 2. Of those that a mesh axis runs over, the one named last changes fastest.
Arguments:
- x_rows: bfloat16 [131072, 1024], P(('dp', 'expert')), may hold values from -24 to 24
- dy_rows: bfloat16 [131072, 2048], P(('dp', 'expert')), may hold values from -0.0234375 to 0.0234375
- seg_blocks: int32 [256, 8], replicated, may hold values from 0 to 2, as said below
Outputs:
- expert_grad: float32 [8, 1024, 2048], P(None, 'dp', 'expert')
Inputs may be any that keep to these rules, and one draw needn't show every extreme that they name: `seg_blocks`: on every device the entries sum to at most 4; one expert has exactly 2 blocks on every device.
All inputs are finite; a program needn't handle non-finite values.
Results may differ from a plain program's by a relative error of at most 0.0003.
Values may be sent and summed in bfloat16 or wider, within the bound.
A program may use at most 128 MiB of HBM per device.

v0:
```python
import jax
import jax.numpy as jnp
from jax import lax
from jax.sharding import PartitionSpec as P

BLOCK = 128
CAP = 2


def contract(left, right):
    return lax.dot_general(
        left, right, (((0,), (0,)), ((), ())), preferred_element_type=jnp.float32
    )


def shards(x_rows, dy_rows, seg_blocks):
    rows, hid = x_rows.shape
    ffn = dy_rows.shape[1]
    n_exp = lax.axis_size("expert")
    n_dp = lax.axis_size("dp")
    experts = seg_blocks.shape[1]
    nblk = rows // BLOCK
    device = lax.axis_index(("dp", "expert"))
    counts = lax.dynamic_slice(seg_blocks, (device, 0), (1, experts))[0]
    starts = jnp.cumsum(counts) - counts
    slots = jnp.arange(CAP, dtype=jnp.int32)
    live = slots[None, :] < counts[:, None]
    index = jnp.where(live, starts[:, None] + slots[None, :], 0).reshape(-1)
    keep = live.reshape(-1)[:, None, None]
    xsend = jnp.where(keep, x_rows.reshape(nblk, BLOCK, hid)[index], jnp.zeros((), x_rows.dtype))
    dysend = jnp.where(keep, dy_rows.reshape(nblk, BLOCK, ffn)[index], jnp.zeros((), dy_rows.dtype))
    xsend = xsend.reshape(experts, CAP * BLOCK, hid)
    dysend = dysend.reshape(experts, CAP * BLOCK, ffn)
    got_x, got_dy = (
        lax.all_to_all(xsend, "expert", split_axis=0, concat_axis=0, tiled=True),
        lax.all_to_all(dysend, "expert", split_axis=0, concat_axis=0, tiled=True),
    )
    got_x = got_x.reshape(n_exp * CAP * BLOCK, hid)
    got_dy = got_dy.reshape(n_exp * CAP * BLOCK, ffn)
    summed = lax.psum_scatter(contract(got_x, got_dy), "dp", scatter_dimension=0, tiled=True)
    return lax.all_to_all(
        summed.reshape(1, hid // n_dp, ffn), "expert", split_axis=2, concat_axis=0, tiled=True
    )


def solution(mesh):
    in_specs = (P(("dp", "expert"), None), P(("dp", "expert"), None), P())
    out_specs = P(None, "dp", "expert")
    return jax.shard_map(shards, mesh=mesh, in_specs=in_specs, out_specs=out_specs, check_vma=False)
```

profile of v0, /device:TPU:8, one launch (start us, length us, event | category | flops | bytes accessed | tf_op | source)
XLA Modules:
  0.0 380.1 jit_solution(2443288582051426192)
XLA Ops:
  6.5 0.0 copy-start
  6.5 1.0 dynamic-slice_reduce_fusion
  7.6 0.1 iota_compare_fusion
  7.6 0.2 reduce-window.8
  7.8 0.1 add_select_fusion
  7.9 0.1 select_n.41
  8.0 0.1 copy.9
  8.1 0.1 broadcast_bitcast_fusion
  8.2 4.0 %gather_fusion = bf16[16,128,1024]{2,1,0:T(8,128)(2,1)} fusion(bf16[4,128,1024]{2,1,0:T(8,128)(2,1)} %bitcast.27, s32[1024]{0:T(1024)S(1)} %pad_clamp_fusion), kind=kCustom, calls=%fused_computation | custom fusion | bytes 8388672 | tf_op jit(solution)/shard_map/gather | solution.py:30
  12.1 6.5 %copy.10 = bf16[8,256,1024]{1,2,0:T(8,128)(2,1)} copy(bf16[8,256,1024]{2,1,0:T(8,128)(2,1)} %bitcast.26) | data formatting | bytes 8388608 | tf_op jit(solution)/shard_map/gather | solution.py:30
  18.6 4.4 %broadcast_select_fusion = bf16[8,256,1024]{1,2,0:T(8,128)(2,1)} fusion(bf16[8,256,1024]{1,2,0:T(8,128)(2,1)} %copy.10, pred[8,256]{1,0:T(8,128)(4,1)S(1)} %broadcast_bitcast_fusion), kind=kLoop, calls=%fused_computation.4 | loop fusion | flops 2097152 | bytes 8390656 | tf_op jit(solution)/shard_map/jit(_where)/select_n | solution.py:30
  23.0 6.6 %all-to-all-start = ((bf16[8,256,1024]{1,2,0:T(8,128)(2,1)}), bf16[8,256,1024]{1,2,0:T(8,128)(2,1)}, u32[]{:S(2)}, u32[]{:S(2)}) async-start(bf16[8,256,1024]{1,2,0:T(8,128)(2,1)} %broadcast_select_fusion), calls=%async_computation | async-start | bytes 8388608 | tf_op jit(solution)/shard_map/all_to_all | solution.py:35
  29.6 0.0 reduce-scatter.2.cloned.1.call-start
  29.6 0.0 copy-done
  29.6 4.6 %gather_fusion.1 = bf16[16,128,2048]{2,1,0:T(8,128)(2,1)} fusion(bf16[4,128,2048]{2,1,0:T(8,128)(2,1)S(1)} %bitcast.24, s32[1024]{0:T(1024)S(1)} %pad_clamp_fusion), kind=kCustom, calls=%fused_computation.1 | custom fusion | bytes 16777280 | tf_op jit(solution)/shard_map/gather | solution.py:31
  34.2 7.3 %bitcast_select_fusion = bf16[8,256,2048]{2,1,0:T(8,128)(2,1)} fusion(pred[8,256]{1,0:T(8,128)(4,1)S(1)} %broadcast_bitcast_fusion, bf16[8,256,2048]{2,1,0:T(8,128)(2,1)} %bitcast.25), kind=kLoop, calls=%fused_computation.2 | loop fusion | flops 4194304 | bytes 16779264 | tf_op jit(solution)/shard_map/jit(_where)/select_n | solution.py:31
  41.5 34.9 %all-to-all-done = bf16[8,256,1024]{1,2,0:T(8,128)(2,1)} async-done(((bf16[8,256,1024]{1,2,0:T(8,128)(2,1)}), bf16[8,256,1024]{1,2,0:T(8,128)(2,1)}, u32[]{:S(2)}, u32[]{:S(2)}) %all-to-all-start) | async-done | bytes 4194336 | tf_op jit(solution)/shard_map/all_to_all | solution.py:35
  76.3 98.9 %all_to_all.28 = bf16[8,256,2048]{2,1,0:T(8,128)(2,1)S(1)} all-to-all(bf16[8,256,2048]{2,1,0:T(8,128)(2,1)} %bitcast_select_fusion), channel_id=1, replica_groups=mesh['dp'=32,'expert'=8] {'expert'}, dimensions={0} | all-to-all | bytes 16777216 | tf_op jit(solution)/shard_map/all_to_all | solution.py:36
  175.2 12.8 %convolution_bitcast_fusion = f32[1024,2048]{1,0:T(8,128)} fusion(bf16[8,256,1024]{1,2,0:T(8,128)(2,1)} %all-to-all-done, bf16[8,256,2048]{2,1,0:T(8,128)(2,1)S(1)} %all_to_all.28), kind=kOutput, calls=%fused_computation.3 | convolution fusion | flops 8589934592 | bytes 20971520 | tf_op jit(solution)/shard_map/dot_general | solution.py:11
  188.0 0.0 reduce-scatter.2.cloned.1.call-update
  188.0 156.4 %reduce-scatter.2.cloned.1.call-done = f32[32,2048]{1,0:T(8,128)} async-done(((f32[1024,2048]{1,0:T(8,128)}), f32[32,2048]{1,0:T(8,128)}) %reduce-scatter.2.cloned.1.call-update) | async-done | bytes 262160 | tf_op jit(solution)/shard_map/reduce_scatter | solution.py:40
  344.4 2.1 copy.11
  346.5 0.5 broadcast.54
  347.1 10.3 %reduce.3 = f32[2048,32]{1,0:T(8,128)} reduce(f32[2048,1,32]{2,1,0:T(1,128)S(1)} %bitcast.28, f32[]{:T(128)} %broadcast.54), dimensions={1}, to_apply=%bitcast.19.reduce_sub_computation | reduce | bytes 524292
  357.4 1.7 reshape.143
  359.1 10.1 %all_to_all.29 = f32[8,1,8192]{2,1,0:T(1,128)S(1)} all-to-all(f32[8,1,8192]{2,1,0:T(1,128)S(1)} %reshape.143), channel_id=1, replica_groups=mesh['dp'=32,'expert'=8] {'expert'}, dimensions={0} | all-to-all | bytes 524288 | tf_op jit(solution)/shard_map/all_to_all | solution.py:41
  369.2 1.3 reduce.4
  370.4 1.8 reshape.144
  372.3 1.0 copy.12
  (3 shorter events, 0.0 us)
Async XLA Ops:
  6.5 23.1 %copy-start = (bf16[512,2048]{1,0:T(8,128)(2,1)S(1)}, bf16[512,2048]{1,0:T(8,128)(2,1)}, u32[]{:S(2)}) copy-start(bf16[512,2048]{1,0:T(8,128)(2,1)} %param.4) | copy-start | bytes 6291460
  23.0 53.3 %all-to-all-start = ((bf16[8,256,1024]{1,2,0:T(8,128)(2,1)}), bf16[8,256,1024]{1,2,0:T(8,128)(2,1)}, u32[]{:S(2)}, u32[]{:S(2)}) async-start(bf16[8,256,1024]{1,2,0:T(8,128)(2,1)} %broadcast_select_fusion), calls=%async_computation | async-start | bytes 8388608 | tf_op jit(solution)/shard_map/all_to_all | solution.py:35
  29.6 314.8 %reduce-scatter.2.cloned.1.call-start = ((), (), s32[]{:S(2)}) async-start(), calls=%async_computation.4 | async-start | bytes 8650752 | tf_op jit(solution)/shard_map/reduce_scatter | solution.py:40
Sparse Core Ops, SparseCore 0:
  188.1 156.2 reduce-scatter.1
where the time goes:
time: 381 us; the launch traced here: 380 us
  waiting for transfers between devices  191 us (50%)
  blocking collectives  109 us (29%)
  other arithmetic  23.6 us (6%)
  local copies, waits for them, and re-layouts  23.4 us (6%)
  between operations  13.4 us (4%)
  matrix products  12.8 us (3%)
  starting transfers between devices  6.58 us (2%)
    reduce_scatter x1, waiting for transfers between devices, shards(): lax.psum_scatter(contract(got_x, got_dy), 'dp', scatter_dimension=0, tile...  156 us
    all_to_all x1, blocking collectives, shards(): lax.all_to_all(dysend, 'expert', split_axis=0, concat_axis=0, tiled=True)  98.9 us
    all_to_all x1, waiting for transfers between devices, shards(): lax.all_to_all(xsend, 'expert', split_axis=0, concat_axis=0, tiled=True)  34.9 us
    dot_general x1, matrix products, contract(): lax.dot_general(left, right, (((0,), (0,)), ((), ())), preferred_element_...  12.8 us
    gather x2, local copies, waits for them, and re-layouts, shards(): x_rows.reshape(nblk, BLOCK, hid)[index]  10.4 us
    unnamed x1, other arithmetic  10.3 us
    all_to_all x1, blocking collectives, shards(): lax.all_to_all(summed.reshape(1, hid // n_dp, ffn), 'expert', split_axis=...  10.1 us
  transfers between devices with their start and end apart: 2, of which 2 were waited for; matrix products, arithmetic and copies ran while one was open for 3% of the time, Pallas kernels for 0%

commit v1 on v0

v1 whole, which is shorter than its diff:
```python
import jax
import jax.numpy as jnp
from jax import lax
from jax.sharding import PartitionSpec as P

BLOCK = 128


def row_owners(seg_blocks, devices, nblk):
    counts = seg_blocks[devices]
    ends = jnp.cumsum(counts, axis=1)
    block = jnp.arange(nblk, dtype=jnp.int32)
    return jnp.sum((ends[:, None, :] <= block[None, :, None]).astype(jnp.int32), axis=2)


def shards(x_rows, dy_rows, seg_blocks):
    rows, hid = x_rows.shape
    ffn = dy_rows.shape[1]
    n_exp = lax.axis_size("expert")
    experts = seg_blocks.shape[1]
    nblk = rows // BLOCK
    devices = lax.axis_index("dp") * n_exp + jnp.arange(n_exp)
    owner = row_owners(seg_blocks, devices, nblk).reshape(-1)
    mask = (owner[None, :] == jnp.arange(experts)[:, None]).astype(x_rows.dtype)
    mask = jnp.repeat(mask, BLOCK, axis=1)
    xg = lax.all_gather(x_rows, "expert", axis=0, tiled=True)
    dyg = lax.all_to_all(dy_rows, "expert", split_axis=1, concat_axis=0, tiled=True)
    xm = (xg[None] * mask[:, :, None])
    part = jnp.einsum("eth,tf->ehf", xm, dyg, preferred_element_type=jnp.float32)
    return lax.psum_scatter(part, "dp", scatter_dimension=1, tiled=True)


def solution(mesh):
    in_specs = (P(("dp", "expert"), None), P(("dp", "expert"), None), P())
    out_specs = P(None, "dp", "expert")
    return jax.shard_map(shards, mesh=mesh, in_specs=in_specs, out_specs=out_specs, check_vma=False)
```

time: 381 us -> 319 us (0.84)
  blocking collectives: 109 us -> 0 us
  waiting for transfers between devices: 191 us -> 260 us
  other arithmetic: 23.6 us -> 0.39 us
  matrix products: 12.8 us -> 22.7 us
  local copies, waits for them, and re-layouts: 23.4 us -> 15.8 us
    all_to_all x2 -> x0, blocking collectives: 109 us -> none  [the longest x1 98.9 us: shards(): lax.all_to_all(dysend, 'expert', split_axis=0, concat_axis=0, tiled=True)]
    all_gather x0 -> x1, waiting for transfers between devices: none -> 102 us  [shards(): xg = lax.all_gather(x_rows, 'expert', axis=0, tiled=True)]
    all_to_all x1, waiting for transfers between devices: 34.9 us -> 0.01 us  [shards(): lax.all_to_all(dy_rows, 'expert', split_axis=1, concat_axis=0, tiled=True)]
    gather x3 -> x1, local copies, waits for them, and re-layouts: 15 us -> 0.56 us  [row_owners(): counts = seg_blocks[devices]]
    all_gather x0 -> x1, local copies, waits for them, and re-layouts: none -> 11.8 us  [shards(): xg = lax.all_gather(x_rows, 'expert', axis=0, tiled=True)]
    select_n x4 -> x1, other arithmetic: 11.8 us -> 0.01 us  [row_owners(): counts = seg_blocks[devices]]
    unnamed x1 -> x0, other arithmetic: 10.3 us -> none
    dot_general x1, matrix products: 12.8 us -> 22.7 us  [shards(): jnp.einsum('eth,tf->ehf', xm, dyg, preferred_element_type=jnp.float32)]
  transfers between devices with their start and end apart: 2 -> 3, of which waited for: 2 -> 2; matrix products, arithmetic and copies ran while one was open for 3% -> 5% of each run, Pallas kernels for 0% -> 0%
where the time goes in v1:
time: 319 us
  waiting for transfers between devices  260 us (82%)
  matrix products  22.7 us (7%)
  local copies, waits for them, and re-layouts  15.8 us (5%)
  between operations  13.4 us (4%)
  starting transfers between devices  5.85 us (2%)
    reduce_scatter x1, waiting for transfers between devices, shards(): return lax.psum_scatter(part, 'dp', scatter_dimension=1, tiled=True)  158 us
    all_gather x1, waiting for transfers between devices, shards(): xg = lax.all_gather(x_rows, 'expert', axis=0, tiled=True)  102 us
    dot_general x1, matrix products, shards(): jnp.einsum('eth,tf->ehf', xm, dyg, preferred_element_type=jnp.float32)  22.7 us
    all_gather x1, local copies, waits for them, and re-layouts, shards(): xg = lax.all_gather(x_rows, 'expert', axis=0, tiled=True)  11.8 us
  transfers between devices with their start and end apart: 3, of which 2 were waited for; matrix products, arithmetic and copies ran while one was open for 5% of the time, Pallas kernels for 0%

profile of v1, /device:TPU:8, one launch (start us, length us, event | category | flops | bytes accessed | tf_op | source)
XLA Modules:
  0.0 318.6 jit_solution(7816214932795877325)
XLA Ops:
  6.5 0.0 copy-start
  6.5 0.0 all-gather.2.cloned.1.call-start
  6.5 0.7 all-gather.2.cloned.1.call-update
  7.3 3.1 copy.16
  10.3 5.8 %all-to-all-start = ((bf16[512,8,256]{2,0,1:T(8,128)(2,1)}), bf16[512,8,256]{2,0,1:T(8,128)(2,1)S(1)}, u32[]{:S(2)}, u32[]{:S(2)}) async-start(bf16[512,8,256]{2,0,1:T(8,128)(2,1)} %bitcast.13), calls=%async_computation | async-start | bytes 4194304 | tf_op jit(solution)/shard_map/all_to_all | solution.py:27
  16.2 0.0 reduce-scatter.2.cloned.1.call-start
  16.2 0.0 copy-done
  16.2 0.1 copy.11
  16.3 0.6 gather_fusion
  16.9 0.2 reduce_window_sum.11
  17.1 0.1 convert_reduce_fusion
  17.2 0.1 copy.12
  17.3 0.1 eq.15
  17.4 0.1 fusion.4
  17.4 0.1 broadcast_bitcast_fusion
  17.6 102.1 %all-gather.2.cloned.1.call-done = bf16[4096,1024]{1,0:T(8,128)(2,1)} async-done(((bf16[512,1024]{1,0:T(8,128)(2,1)}), bf16[4096,1024]{1,0:T(8,128)(2,1)}) %all-gather.2.cloned.1.call-update) | async-done | bytes 8388624 | tf_op jit(solution)/shard_map/all_gather | solution.py:26
  119.6 11.8 %copy.10 = bf16[4096,1024]{0,1:T(8,128)(2,1)} copy(bf16[4096,1024]{1,0:T(8,128)(2,1)} %all-gather.2.cloned.1.call-done) | data formatting | bytes 16777216 | tf_op jit(solution)/shard_map/all_gather | solution.py:26
  131.4 0.0 all-to-all-done
  131.4 22.7 %fusion = f32[8,1024,256]{2,1,0:T(8,128)} fusion(bf16[4096,256,1]{1,0,2:T(8,128)(2,1)S(1)} %bitcast.15, bf16[8,4096]{1,0:T(8,128)(2,1)S(1)} %broadcast_bitcast_fusion, bf16[4096,1024]{0,1:T(8,128)(2,1)} %copy.10), kind=kOutput, calls=%fused_computation.1 | convolution fusion | flops 17213423616 | bytes 18939904 | tf_op jit(solution)/shard_map/eth,tf->ehf/dot_general | solution.py:29
  154.2 0.0 reduce-scatter.2.cloned.1.call-update
  154.2 157.6 %reduce-scatter.2.cloned.1.call-done = f32[8,32,256]{2,1,0:T(8,128)} async-done(((f32[8,1024,256]{2,1,0:T(8,128)}), f32[8,32,256]{2,1,0:T(8,128)}) %reduce-scatter.2.cloned.1.call-update) | async-done | bytes 262160 | tf_op jit(solution)/shard_map/reduce_scatter | solution.py:30
  (2 shorter events, 0.0 us)
Async XLA Ops:
  6.5 9.6 %copy-start = (s32[256,8]{0,1:T(8,128)S(1)}, s32[256,8]{0,1:T(8,128)}, u32[]{:S(2)}) copy-start(s32[256,8]{0,1:T(8,128)} %param.5) | copy-start | bytes 24580
  6.5 113.1 %all-gather.2.cloned.1.call-start = ((), (), s32[]{:S(2)}) async-start(), calls=%async_computation.2 | async-start | bytes 9437184 | tf_op jit(solution)/shard_map/all_gather | solution.py:26
  10.3 121.1 %all-to-all-start = ((bf16[512,8,256]{2,0,1:T(8,128)(2,1)}), bf16[512,8,256]{2,0,1:T(8,128)(2,1)S(1)}, u32[]{:S(2)}, u32[]{:S(2)}) async-start(bf16[512,8,256]{2,0,1:T(8,128)(2,1)} %bitcast.13), calls=%async_computation | async-start | bytes 4194304 | tf_op jit(solution)/shard_map/all_to_all | solution.py:27
  16.2 295.6 %reduce-scatter.2.cloned.1.call-start = ((), (), s32[]{:S(2)}) async-start(), calls=%async_computation.3 | async-start | bytes 8650752 | tf_op jit(solution)/shard_map/reduce_scatter | solution.py:30
Sparse Core Ops, SparseCore 0:
  9.1 110.4 all-gather.1
  154.3 157.4 reduce-scatter.1

commit v2 on v1

v2 whole, which is shorter than its diff:
```python
import functools

import jax
import jax.numpy as jnp
from jax import lax
from jax.experimental import pallas as pl
from jax.experimental.pallas import tpu as pltpu
from jax.sharding import PartitionSpec as P

BLOCK = 128
NE = 8
NY, NX, NZ = 4, 4, 8
NG = 2 * NY
HR, FC = 32, 256
HALF = NE // 2
MSG = HALF * HR + 16
OFFS = (4, 3, -3, 2, -2, 1, -1, 0)
QMAX = 32700.0


def encode(dst, scales, get):
    for e in range(HALF):
        v = get(e)
        top = jnp.max(jnp.abs(v), axis=0, keepdims=True)
        lev = jnp.ceil(jnp.log2(jnp.maximum(top, 1e-30)) * 256.0) + 1.0
        q = jnp.round(v * (jnp.exp2(lev * (-1.0 / 256.0)) * QMAX))
        dst[e * HR:(e + 1) * HR, :] = q.astype(jnp.int32).astype(jnp.int16)
        scales[e:e + 1, :] = lev
    dst[HALF * HR:, :] = scales[...].astype(jnp.int32).astype(jnp.int16)


def decoder(src):
    lev = src[HALF * HR:, :].astype(jnp.int32).astype(jnp.float32)
    s = jnp.exp2(lev * (1.0 / 256.0)) * (1.0 / QMAX)

    def get(e):
        q = src[e * HR:(e + 1) * HR, :].astype(jnp.int32).astype(jnp.float32)
        return q * s[e:e + 1, :]
    return get


def kernel(xt, dy, msk, out, xg, dyg, rel, part, xa_s, xa_r, xb_s, xb_r, z_s, z_r, scales,
           dsem, xsem, asem, bsem, zsem):
    dp, ex = lax.axis_index("dp"), lax.axis_index("expert")
    z, xh, c = dp // 4, (dp // 2) % 2, dp % 2
    xl, y = ex // NY, ex % NY
    X = xh * 2 + xl

    def at(z_=z, x_=X, c_=c, y_=y):
        return (z_ * 4 + (x_ // 2) * 2 + c_, (x_ % 2) * NY + y_)

    yp, ym = (y + 1) % NY, (y + 3) % NY
    xp, xm = (X + 1) % NX, (X + 3) % NX
    zp, zm = (z + 1) % NZ, (z + 7) % NZ
    partner = at(c_=1 - c)
    up, down = at(y_=yp), at(y_=ym)
    right, left = at(x_=xp), at(x_=xm)
    ahead, behind = at(z_=zp), at(z_=zm)
    g_me, g_pa = y * 2 + c, y * 2 + 1 - c

    barrier = pltpu.get_barrier_semaphore()
    for other in (partner, up, down, right, left, ahead, behind):
        pl.semaphore_signal(barrier, inc=1, device_id=other, device_id_type=pl.DeviceIdType.MESH)
    scales[...] = jnp.zeros_like(scales)
    pl.semaphore_wait(barrier, 7)

    started = []

    def copy(src, dst, sem, dev):
        return pltpu.make_async_remote_copy(
            src_ref=src, dst_ref=dst, send_sem=sem.at[0], recv_sem=sem.at[1],
            device_id=dev, device_id_type=pl.DeviceIdType.MESH)

    def send(src, dst, sem, dev):
        op = copy(src, dst, sem, dev)
        op.start()
        started.append(op)

    def arrived(dst, sem):
        copy(dst, dst, sem, partner).wait_recv()

    def cols(yy, j):
        return dy.at[:, pl.ds(pl.multiple_of((j * NY + yy) * FC, FC), FC)]

    y2 = (y + 2) % NY
    send(cols(y2, 0), rel.at[0], dsem.at[0], up)
    send(cols(y2, 1), rel.at[1], dsem.at[1], down)
    send(xt.at[1 - c], xg.at[g_me], xsem.at[48], partner)
    for j in range(2):
        send(cols(yp, j), dyg.at[g_me, j], dsem.at[2 + j], up)
        send(cols(ym, j), dyg.at[g_me, j], dsem.at[4 + j], down)
        send(cols(y, j), dyg.at[g_me, j], dsem.at[6 + j], partner)
    for j in range(2):
        dyg[g_me, j] = dy[:, pl.ds(pl.multiple_of((j * NY + y) * FC, FC), FC)]
    xg[g_me] = xt[c]
    arrived(xg.at[g_pa], xsem.at[48])

    def zof(k):
        return (z + OFFS[k] + NZ) % NZ

    def xsend(k):
        zk = zof(k)
        for i, (s, g) in enumerate(((xt.at[c, zk], g_me), (xg.at[g_pa, zk], g_pa))):
            send(s, xg.at[g, zk], xsem.at[k * 6 + i], up)
            send(s, xg.at[g, zk], xsem.at[k * 6 + 2 + i], down)

    def xforward(k):
        zk = zof(k)
        for i in range(2):
            g_d, g_u = ym * 2 + (c if i == 0 else 1 - c), yp * 2 + (c if i == 0 else 1 - c)
            arrived(xg.at[g_d, zk], xsem.at[k * 6 + i])
            arrived(xg.at[g_u, zk], xsem.at[k * 6 + 2 + i])
        send(xg.at[ym * 2 + c, zk], xg.at[ym * 2 + c, zk], xsem.at[k * 6 + 4], up)
        send(xg.at[yp * 2 + 1 - c, zk], xg.at[yp * 2 + 1 - c, zk], xsem.at[k * 6 + 5], down)

    xsend(0)
    arrived(rel.at[0], dsem.at[0])
    send(rel.at[0], dyg.at[ym * 2 + c, 0], dsem.at[8], up)
    arrived(rel.at[1], dsem.at[1])
    send(rel.at[1], dyg.at[yp * 2 + c, 1], dsem.at[9], down)
    xsend(1)
    gd, gu, gf = ym * 2 + c, yp * 2 + c, y2 * 2 + c
    for n, (g, j, s) in enumerate(((gd, 0, 2), (gu, 0, 4), (gd, 1, 3), (gu, 1, 5))):
        arrived(dyg.at[g, j], dsem.at[s])
        send(dyg.at[g, j], dyg.at[g, j], dsem.at[10 + n], partner)
    xforward(0)
    for n, (g, j, s) in enumerate(((gf, 0, 8), (gf, 1, 9))):
        arrived(dyg.at[g, j], dsem.at[s])
        send(dyg.at[g, j], dyg.at[g, j], dsem.at[14 + n], partner)
    pd, pu, pf = ym * 2 + 1 - c, yp * 2 + 1 - c, y2 * 2 + 1 - c
    for g, j, s in ((g_pa, 0, 6), (g_pa, 1, 7), (pd, 0, 10), (pu, 0, 11), (pd, 1, 12), (pu, 1, 13), (pf, 0, 14), (pf, 1, 15)):
        arrived(dyg.at[g, j], dsem.at[s])

    def multiply(k, b, hh):
        zk = zof(k)
        for j in range(2):
            part[b, hh * 2 + j] = jnp.zeros((NE * HR, FC), jnp.float32)

        def step(g, _):
            v = xg[g, zk, hh]
            m = msk[g]
            lhs = jnp.concatenate([v * m[e:e + 1, :] for e in range(NE)], axis=0)
            for j in range(2):
                part[b, hh * 2 + j] += jnp.dot(lhs, dyg[g, j], preferred_element_type=jnp.float32)
            return 0
        lax.fori_loop(0, NG, step, 0)

    def rows(b, x_, h):
        return lambda e: part[b, x_, (h * HALF + e) * HR:(h * HALF + e + 1) * HR, :]

    def plus(*gets):
        return lambda e: functools.reduce(lambda p, q: p + q, [g(e) for g in gets])

    def compute(k):
        b = k % 3
        multiply(k, b, 1 - xh)
        opp = (X + 2) % NX
        encode(xa_s.at[k, 0], scales, rows(b, opp, 0))
        send(xa_s.at[k, 0], xa_r.at[k, 0], asem.at[k * 2], right)
        encode(xa_s.at[k, 1], scales, rows(b, opp, 1))
        send(xa_s.at[k, 1], xa_r.at[k, 1], asem.at[k * 2 + 1], left)
        multiply(k, b, xh)
        encode(xb_s.at[k, 0, 1], scales, rows(b, xp, 1))
        send(xb_s.at[k, 0, 1], xb_r.at[k, 0, 1], bsem.at[k * 4 + 1], right)
        encode(xb_s.at[k, 1, 0], scales, rows(b, xm, 0))
        send(xb_s.at[k, 1, 0], xb_r.at[k, 1, 0], bsem.at[k * 4 + 2], left)

    def xsum(k):
        b = k % 3
        arrived(xa_r.at[k, 0], asem.at[k * 2])
        encode(xb_s.at[k, 0, 0], scales, plus(rows(b, xp, 0), decoder(xa_r.at[k, 0])))
        send(xb_s.at[k, 0, 0], xb_r.at[k, 0, 0], bsem.at[k * 4], right)
        arrived(xa_r.at[k, 1], asem.at[k * 2 + 1])
        encode(xb_s.at[k, 1, 1], scales, plus(rows(b, xm, 1), decoder(xa_r.at[k, 1])))
        send(xb_s.at[k, 1, 1], xb_r.at[k, 1, 1], bsem.at[k * 4 + 3], left)

    def zsum(k):
        b, off = k % 3, OFFS[k]
        for i in range(2):
            for h in range(2):
                arrived(xb_r.at[k, i, h], bsem.at[k * 4 + i * 2 + h])
        terms = []
        for h in range(2):
            terms.append([rows(b, X, h), decoder(xb_r.at[k, 0, h]), decoder(xb_r.at[k, 1, h])])
        if off == 3:
            arrived(z_r.at[k, 0, 0], zsem.at[k * 2])
            terms[0].append(decoder(z_r.at[k, 0, 0]))
        elif off == -3:
            arrived(z_r.at[k, 1, 1], zsem.at[k * 2 + 1])
            terms[1].append(decoder(z_r.at[k, 1, 1]))
        else:
            for i in range(2):
                if (i == 0 and off in (2, 1, 0)) or (i == 1 and off in (-2, -1, 0)):
                    arrived(z_r.at[k, i], zsem.at[k * 2 + i])
                    for h in range(2):
                        terms[h].append(decoder(z_r.at[k, i, h]))
        if off == 0:
            for h in range(2):
                get = plus(*terms[h])
                for e in range(HALF):
                    out[h * HALF + e] = get(e)
            return
        for h in range(2):
            encode(z_s.at[k, h], scales, plus(*terms[h]))
        if off == 4:
            send(z_s.at[k, 0], z_r.at[1, 0, 0], zsem.at[1 * 2], ahead)
            send(z_s.at[k, 1], z_r.at[2, 1, 1], zsem.at[2 * 2 + 1], behind)
        elif off > 0:
            n = OFFS.index(off - 1)
            send(z_s.at[k], z_r.at[n, 0], zsem.at[n * 2], ahead)
        else:
            n = OFFS.index(off + 1)
            send(z_s.at[k], z_r.at[n, 1], zsem.at[n * 2 + 1], behind)

    for k in range(NZ):
        if k + 2 < NZ:
            xsend(k + 2)
        if k + 1 < NZ:
            xforward(k + 1)
        zk = zof(k)
        arrived(xg.at[y2 * 2 + c, zk], xsem.at[k * 6 + 4])
        arrived(xg.at[y2 * 2 + 1 - c, zk], xsem.at[k * 6 + 5])
        compute(k)
        if k >= 1:
            xsum(k - 1)
        if k >= 2:
            zsum(k - 2)
    xsum(NZ - 1)
    zsum(NZ - 2)
    zsum(NZ - 1)
    for op in started:
        op.wait_send()


def shards(x_rows, dy_rows, seg_blocks):
    rows, hid = x_rows.shape
    nblk = rows // BLOCK
    dp, ex = lax.axis_index("dp"), lax.axis_index("expert")
    g = jnp.arange(NG)
    devices = ((dp // 2) * 2 + g % 2) * NG + (ex // NY) * NY + g // 2
    ends = jnp.cumsum(seg_blocks[devices], axis=1)
    block = jnp.arange(nblk, dtype=jnp.int32)
    owner = jnp.sum((ends[:, None, :] <= block[None, :, None]).astype(jnp.int32), axis=2)
    mask = (owner[:, None, :] == jnp.arange(NE)[None, :, None]).astype(x_rows.dtype)
    mask = jnp.repeat(mask, BLOCK, axis=2)
    xt = x_rows.T.reshape(NZ, 2, 2, HR, rows).transpose(2, 0, 1, 3, 4)
    vm = pl.BlockSpec(memory_space=pltpu.VMEM)
    i16 = jnp.int16
    return pl.pallas_call(
        kernel,
        out_shape=jax.ShapeDtypeStruct((NE, HR, FC), jnp.float32),
        in_specs=[vm] * 3,
        out_specs=vm,
        scratch_shapes=[
            pltpu.VMEM((NG, NZ, 2, HR, rows), x_rows.dtype),
            pltpu.VMEM((NG, 2, rows, FC), x_rows.dtype),
            pltpu.VMEM((2, rows, FC), x_rows.dtype),
            pltpu.VMEM((3, 4, NE * HR, FC), jnp.float32),
            pltpu.VMEM((NZ, 2, MSG, FC), i16),
            pltpu.VMEM((NZ, 2, MSG, FC), i16),
            pltpu.VMEM((NZ, 2, 2, MSG, FC), i16),
            pltpu.VMEM((NZ, 2, 2, MSG, FC), i16),
            pltpu.VMEM((NZ, 2, MSG, FC), i16),
            pltpu.VMEM((NZ, 2, 2, MSG, FC), i16),
            pltpu.VMEM((16, FC), jnp.float32),
            pltpu.SemaphoreType.DMA((16, 2)),
            pltpu.SemaphoreType.DMA((49, 2)),
            pltpu.SemaphoreType.DMA((16, 2)),
            pltpu.SemaphoreType.DMA((32, 2)),
            pltpu.SemaphoreType.DMA((16, 2)),
        ],
        compiler_params=pltpu.CompilerParams(
            collective_id=0, has_side_effects=True, vmem_limit_bytes=56 << 20),
    )(xt, dy_rows, mask)


def solution(mesh):
    in_specs = (P(("dp", "expert"), None), P(("dp", "expert"), None), P())
    out_specs = P(None, "dp", "expert")
    return jax.shard_map(shards, mesh=mesh, in_specs=in_specs, out_specs=out_specs, check_vma=False)
```

time: 319 us -> 104 us (0.33)
  waiting for transfers between devices: 260 us -> 0 us
  Pallas kernels: 0 us -> 96.2 us
  matrix products: 22.7 us -> 0 us
  between operations: 13.4 us -> 0.07 us
  local copies, waits for them, and re-layouts: 15.8 us -> 5.75 us
  starting transfers between devices: 5.85 us -> 0 us
    reduce_scatter x1 -> x0, waiting for transfers between devices: 158 us -> none  [shards(): return lax.psum_scatter(part, 'dp', scatter_dimension=1, tiled=True)]
    all_gather x1 -> x0, waiting for transfers between devices: 102 us -> none  [shards(): xg = lax.all_gather(x_rows, 'expert', axis=0, tiled=True)]
    pallas_call x0 -> x1, Pallas kernels: none -> 96.2 us  [shards(): pl.pallas_call(kernel, out_shape=jax.ShapeDtypeStruct((NE, HR, FC), jnp.f...]
    dot_general x1 -> x0, matrix products: 22.7 us -> none  [shards(): jnp.einsum('eth,tf->ehf', xm, dyg, preferred_element_type=jnp.float32)]
    all_gather x1 -> x0, local copies, waits for them, and re-layouts: 11.8 us -> none  [shards(): xg = lax.all_gather(x_rows, 'expert', axis=0, tiled=True)]
    all_to_all x1 -> x0, starting transfers between devices: 5.84 us -> none  [shards(): lax.all_to_all(dy_rows, 'expert', split_axis=1, concat_axis=0, tiled=True)]
  transfers between devices with their start and end apart: 3 -> 0, of which waited for: 2 -> 0; matrix products, arithmetic and copies ran while one was open for 5% -> 0% of each run, Pallas kernels for 0% -> 0%
where the time goes in v2:
time: 104 us; the launch traced here: 102 us
  Pallas kernels  96.2 us (92%)
  local copies, waits for them, and re-layouts  5.75 us (6%)
    pallas_call x1, Pallas kernels, shards(): pl.pallas_call(kernel, out_shape=jax.ShapeDtypeStruct((NE, HR, FC), jnp.f...  96.2 us
    unnamed x5, local copies, waits for them, and re-layouts  3.3 us

profile of v2, /device:TPU:8, one launch (start us, length us, event | category | flops | bytes accessed | tf_op | source)
XLA Modules:
  0.0 102.5 jit_solution(12170016986722540217)
XLA Ops:
  0.0 0.0 copy-start
  0.0 1.5 %copy.8 = bf16[512,1024]{0,1:T(8,128)(2,1)S(1)} copy(bf16[512,1024]{1,0:T(8,128)(2,1)} %param.3) | data formatting | bytes 2097152 | tf_op args[0]
  1.5 1.1 %copy.13 = bf16[8,2,2,32,512]{4,3,1,0,2:T(8,128)(2,1)} copy(bf16[8,2,2,32,512]{4,3,2,1,0:T(8,128)(2,1)S(1)} %bitcast.11) | data formatting | bytes 2097152 | tf_op jit(solution)/shard_map/reshape | solution.py:246
  2.6 0.0 copy-done
  2.6 0.1 copy.10
  2.8 0.6 gather_fusion
  3.3 0.2 reduce_window_sum.11
  3.5 0.1 convert_reduce_fusion
  3.6 0.1 copy.11
  3.7 0.1 fusion
  3.8 0.7 broadcast_bitcast_fusion.msk
  4.5 96.2 %shard_map.37 = f32[8,32,256]{2,1,0:T(8,128)} custom-call(bf16[2,8,2,32,512]{4,3,2,1,0:T(8,128)(2,1)} %bitcast.10, bf16[512,2048]{1,0:T(8,128)(2,1)} %dy.1, bf16[8,8,512]{2,1,0:T(8,128)(2,1)} %broadcast_bitcast_fusion.msk), custom_call_target="tpu_custom_call" | custom-call | tf_op jit(solution)/shard_map/pallas_call | solution.py:249
  100.8 1.7 %copy.15 = f32[8,32,256]{2,1,0:T(8,128)} copy(f32[8,32,256]{2,1,0:T(8,128)} %shard_map.37) | data formatting | bytes 524288
  (2 shorter events, 0.0 us)
Async XLA Ops:
  0.0 2.6 %copy-start = (s32[256,8]{0,1:T(8,128)S(1)}, s32[256,8]{0,1:T(8,128)}, u32[]{:S(2)}) copy-start(s32[256,8]{0,1:T(8,128)} %param.5) | copy-start | bytes 24580

commit v3 on v1

v3 whole, which is shorter than its diff:
```python
import functools

import jax
import jax.numpy as jnp
from jax import lax
from jax.experimental import pallas as pl
from jax.experimental.pallas import tpu as pltpu
from jax.sharding import PartitionSpec as P

BLOCK = 128
NE = 8
NC = NE - 1
NB = (4, 3)
TOK = 2 * BLOCK
NY, NX, NZ = 4, 4, 8
NG = 2 * NY
GG = 4
HR, FC = 32, 256
MSG = 4 * HR + 16
OFFS = (4, 3, -3, 2, -2, 1, -1, 0)
QMAX = 32700.0


def encode(dst, scales, n, get):
    for e in range(n):
        v = get(e)
        top = jnp.max(jnp.abs(v), axis=0, keepdims=True)
        lev = jnp.ceil(jnp.log2(jnp.maximum(top, 1e-30)) * 256.0) + 1.0
        q = jnp.round(v * (jnp.exp2(lev * (-1.0 / 256.0)) * QMAX))
        dst[e * HR:(e + 1) * HR, :] = q.astype(jnp.int32).astype(jnp.int16)
        scales[e:e + 1, :] = lev
    dst[n * HR:n * HR + 16, :] = scales[...].astype(jnp.int32).astype(jnp.int16)


def decoder(src, n):
    lev = src[n * HR:n * HR + 16, :].astype(jnp.int32).astype(jnp.float32)
    s = jnp.exp2(lev * (1.0 / 256.0)) * (1.0 / QMAX)

    def get(e):
        q = src[e * HR:(e + 1) * HR, :].astype(jnp.int32).astype(jnp.float32)
        return q * s[e:e + 1, :]
    return get


def plus(*gets):
    return lambda e: functools.reduce(lambda p, q: p + q, [g(e) for g in gets])


def span(n):
    return pl.ds(0, n * HR + 16)


def kernel(pos, x, dy, msk, out, xo_h, xo_c, xh_p, xg, dyh_o, dyh_p, dyc, dyg, rel, lhs, part, hp, xa_s, xa_r, xb_s, xb_r,
           z_s, z_r, hz_s, hz_r, hr, hxa_s, hxa_r, hxb_s, hxb_r, hy, hy_s, hy_r, scales,
           dsem, xsem, asem, bsem, zsem, hsem, tsem):
    dp, ex = lax.axis_index("dp"), lax.axis_index("expert")
    z, xh, c = dp // 4, (dp // 2) % 2, dp % 2
    xl, y = ex // NY, ex % NY
    X = xh * 2 + xl

    def at(z_=z, x_=X, c_=c, y_=y):
        return (z_ * 4 + (x_ // 2) * 2 + c_, (x_ % 2) * NY + y_)

    yp, ym, y2 = (y + 1) % NY, (y + 3) % NY, (y + 2) % NY
    xp, xm, x2 = (X + 1) % NX, (X + 3) % NX, (X + 2) % NX
    zp, zm = (z + 1) % NZ, (z + 7) % NZ
    partner = at(c_=1 - c)
    up, down = at(y_=yp), at(y_=ym)
    right, left = at(x_=xp), at(x_=xm)
    ahead, behind = at(z_=zp), at(z_=zm)
    g_me, g_pa = y * 2 + c, y * 2 + 1 - c

    barrier = pltpu.get_barrier_semaphore()
    for other in (partner, up, down, right, left, ahead, behind):
        pl.semaphore_signal(barrier, inc=1, device_id=other, device_id_type=pl.DeviceIdType.MESH)
    scales[...] = jnp.zeros_like(scales)

    def pick(ref, j, i, n):
        a, b = ref[j * BLOCK:(j + 1) * BLOCK, n], ref[(j + 2) * BLOCK:(j + 3) * BLOCK, n]
        m = 2 * j + 1 - i
        return a * pos[m:m + 1, n] + b * pos[2 * j + i:2 * j + i + 1, n]

    for i, dst in ((1, dyc), (0, dyh_o)):
        for j in range(2):
            dst[j * BLOCK:(j + 1) * BLOCK, :] = pick(dy, j, i, slice(0, 8 * FC))
    pl.semaphore_wait(barrier, 7)

    started = []

    def copy(src, dst, sem, dev):
        return pltpu.make_async_remote_copy(
            src_ref=src, dst_ref=dst, send_sem=sem.at[0], recv_sem=sem.at[1],
            device_id=dev, device_id_type=pl.DeviceIdType.MESH)

    def send(src, dst, sem, dev):
        op = copy(src, dst, sem, dev)
        op.start()
        started.append(op)

    def arrived(dst, sem):
        copy(dst, dst, sem, partner).wait_recv()

    def cols(yy, j):
        return pl.ds(pl.multiple_of((j * NY + yy) * FC, FC), FC)

    def dyslot(j, g):
        return dyg.at[j, pl.ds(pl.multiple_of(g * TOK, TOK), TOK)]

    send(dyc.at[:, cols(y2, 0)], rel.at[0], dsem.at[0], up)
    send(dyc.at[:, cols(y2, 1)], rel.at[1], dsem.at[1], down)
    send(dyh_o, dyh_p, tsem.at[0], partner)
    for j in range(2):
        send(dyc.at[:, cols(yp, j)], dyslot(j, g_me), dsem.at[2 + j], up)
        send(dyc.at[:, cols(ym, j)], dyslot(j, g_me), dsem.at[4 + j], down)
        send(dyc.at[:, cols(y, j)], dyslot(j, g_me), dsem.at[6 + j], partner)
    for j in range(2):
        dyg[j, pl.ds(pl.multiple_of(g_me * TOK, TOK), TOK)] = dyc[:, cols(y, j)]

    def turn(n, _):
        for j in range(4):
            t = pick(x, j % 2, j // 2, pl.ds(pl.multiple_of(n * BLOCK, BLOCK), BLOCK)).T
            dst = (xo_h, xo_c)[j // 2]
            for i in range(4):
                dst[i % 2, n, i // 2, :, (j % 2) * BLOCK:(j % 2 + 1) * BLOCK] = t[i * HR:(i + 1) * HR, :]
        return 0
    lax.fori_loop(0, NZ, turn, 0)
    send(xo_h.at[1 - c], xh_p, tsem.at[1], partner)
    send(xo_c.at[1 - c], xg.at[g_me], tsem.at[2], partner)
    xg[g_me] = xo_c[c]

    def zof(k):
        return (z + OFFS[k] + NZ) % NZ

    def xsend(k):
        zk = zof(k)
        for i, (s, g) in enumerate(((xo_c.at[c, zk], g_me), (xg.at[g_pa, zk], g_pa))):
            send(s, xg.at[g, zk], xsem.at[k * 6 + i], up)
            send(s, xg.at[g, zk], xsem.at[k * 6 + 2 + i], down)

    def xforward(k):
        zk = zof(k)
        for i in range(2):
            g_d, g_u = ym * 2 + (c if i == 0 else 1 - c), yp * 2 + (c if i == 0 else 1 - c)
            arrived(xg.at[g_d, zk], xsem.at[k * 6 + i])
            arrived(xg.at[g_u, zk], xsem.at[k * 6 + 2 + i])
        send(xg.at[ym * 2 + c, zk], xg.at[ym * 2 + c, zk], xsem.at[k * 6 + 4], up)
        send(xg.at[yp * 2 + 1 - c, zk], xg.at[yp * 2 + 1 - c, zk], xsem.at[k * 6 + 5], down)

    def hmultiply():
        left_ = jnp.concatenate([xo_h[c].reshape(NZ * 2 * HR, TOK), xh_p[...].reshape(NZ * 2 * HR, TOK)], axis=1)
        for n in range(8):
            r = jnp.concatenate([dyh_o[:, n * FC:(n + 1) * FC], dyh_p[:, n * FC:(n + 1) * FC]], axis=0)
            hp[n] = jnp.dot(left_, r, preferred_element_type=jnp.float32).reshape(NZ, 2, HR, FC)

    def hrows(k, u):
        zk = zof(k)
        return lambda i: hp[(u % 2) * NY + i, zk, u // 2]

    def hstart():
        for u, n, i, dev in ((0, 1, 0, ahead), (2, 2, 1, behind), (1, 1, 0, ahead), (3, 2, 1, behind)):
            encode(hz_s.at[0, u], scales, 4, hrows(0, u))
            send(hz_s.at[0, u], hz_r.at[n, i, u], hsem.at[(n * 2 + i) * 4 + u], dev)

    def hstep(off):
        for t in range(4):
            for i, dev in ((0, ahead), (1, behind)):
                k = OFFS.index(off if i == 0 else -off)
                n = OFFS.index(off - 1 if i == 0 else 1 - off)
                u = ((2, 3, 0, 1) if i == 0 else (0, 1, 2, 3))[t]
                get = hrows(k, u)
                if off < 3 or t >= 2:
                    arrived(hz_r.at[k, i, u], hsem.at[(k * 2 + i) * 4 + u])
                    get = plus(get, decoder(hz_r.at[k, i, u], 4))
                encode(hz_s.at[k, u], scales, 4, get)
                send(hz_s.at[k, u], hz_r.at[n, i, u], hsem.at[(n * 2 + i) * 4 + u], dev)

    def hlast():
        for u in range(4):
            for i in range(2):
                arrived(hz_r.at[7, i, u], hsem.at[(7 * 2 + i) * 4 + u])
            get = plus(hrows(7, u), decoder(hz_r.at[7, 0, u], 4), decoder(hz_r.at[7, 1, u], 4))
            for i in range(4):
                hr[u, i] = get(i)
        encode(hxa_s.at[0], scales, 2, lambda i: hr[x2, i])
        send(hxa_s.at[0, span(2)], hxa_r.at[0, span(2)], tsem.at[3], right)
        encode(hxa_s.at[1], scales, 2, lambda i: hr[x2, 2 + i])
        send(hxa_s.at[1, span(2)], hxa_r.at[1, span(2)], tsem.at[4], left)

    def hx():
        arrived(hxa_r.at[0, span(2)], tsem.at[3])
        arrived(hxa_r.at[1, span(2)], tsem.at[4])
        d0, d1 = decoder(hxa_r.at[0], 2), decoder(hxa_r.at[1], 2)
        encode(hxb_s.at[0], scales, 4, lambda i: hr[xp, i] + d0(i) if i < 2 else hr[xp, i])
        send(hxb_s.at[0], hxb_r.at[0], tsem.at[5], right)
        encode(hxb_s.at[1], scales, 4, lambda i: hr[xm, i] + d1(i - 2) if i >= 2 else hr[xm, i])
        send(hxb_s.at[1], hxb_r.at[1], tsem.at[6], left)

    def hxlast():
        arrived(hxb_r.at[0], tsem.at[5])
        arrived(hxb_r.at[1], tsem.at[6])
        get = plus(lambda i: hr[X, i], decoder(hxb_r.at[0], 4), decoder(hxb_r.at[1], 4))
        for i in range(4):
            hy[i] = get(i)
        send(hy.at[y2], hy_r.at[0], tsem.at[7], up)
        send(hy.at[ym], hy_r.at[2], tsem.at[8], down)

    def hyadd():
        arrived(hy_r.at[0], tsem.at[7])
        hy_s[...] = hy[yp] + hy_r[0]
        send(hy_s, hy_r.at[1], tsem.at[9], up)

    def hylast():
        arrived(hy_r.at[2], tsem.at[8])
        arrived(hy_r.at[1], tsem.at[9])
        out[0] = hy[y] + hy_r[1] + hy_r[2]

    def multiply(k):
        b, zk = k % 3, zof(k)
        for q in range(NG // GG):
            for h in range(2):
                v = jnp.concatenate([xg[q * GG + i, zk, h] for i in range(GG)], axis=1)
                for e in range(NC):
                    lhs[(h * NC + e) * HR:(h * NC + e + 1) * HR, :] = v * msk[q, e:e + 1, :]
            for j in range(2):
                r = jnp.dot(lhs[...], dyg[j, q * GG * TOK:(q + 1) * GG * TOK, :], preferred_element_type=jnp.float32)
                r = r.reshape(2, NC * HR, FC)
                part[b, j] = r if q == 0 else part[b, j] + r

    def rows(k, x_, h):
        return lambda e: part[k % 3, x_ % 2, x_ // 2, (h * 4 + e) * HR:(h * 4 + e + 1) * HR, :]

    def compute(k):
        multiply(k)
        for h, dev in ((0, right), (1, left)):
            encode(xa_s.at[k, h], scales, NB[h], rows(k, x2, h))
            send(xa_s.at[k, h, span(NB[h])], xa_r.at[k, h, span(NB[h])], asem.at[k * 2 + h], dev)
        for i, h, x_, dev in ((0, 1, xp, right), (1, 0, xm, left)):
            encode(xb_s.at[k, i, h], scales, NB[h], rows(k, x_, h))
            send(xb_s.at[k, i, h, span(NB[h])], xb_r.at[k, i, h, span(NB[h])], bsem.at[k * 4 + i * 2 + h], dev)

    def xsum(k):
        for h, x_, dev in ((0, xp, right), (1, xm, left)):
            arrived(xa_r.at[k, h, span(NB[h])], asem.at[k * 2 + h])
            encode(xb_s.at[k, h, h], scales, NB[h], plus(rows(k, x_, h), decoder(xa_r.at[k, h], NB[h])))
            send(xb_s.at[k, h, h, span(NB[h])], xb_r.at[k, h, h, span(NB[h])], bsem.at[k * 4 + h * 2 + h], dev)

    def zsum(k):
        off = OFFS[k]
        for h in range(2):
            n = NB[h]
            for i in range(2):
                arrived(xb_r.at[k, i, h, span(n)], bsem.at[k * 4 + i * 2 + h])
            terms = [rows(k, X, h), decoder(xb_r.at[k, 0, h], n), decoder(xb_r.at[k, 1, h], n)]
            for i in range(2):
                sign = off if i == 0 else -off
                if sign in (0, 1, 2) or (sign == 3 and h == i):
                    arrived(z_r.at[k, i, h, span(n)], zsem.at[(k * 2 + i) * 2 + h])
                    terms.append(decoder(z_r.at[k, i, h], n))
            get = plus(*terms)
            if off == 0:
                for e in range(n):
                    out[1 + h * 4 + e] = get(e)
                continue
            encode(z_s.at[k, h], scales, n, get)
            i = h if off == 4 else (0 if off > 0 else 1)
            m = OFFS.index((3, -3)[i] if off == 4 else (off - 1 if off > 0 else off + 1))
            send(z_s.at[k, h, span(n)], z_r.at[m, i, h, span(n)], zsem.at[(m * 2 + i) * 2 + h], (ahead, behind)[i])

    arrived(rel.at[0], dsem.at[0])
    send(rel.at[0], dyslot(0, ym * 2 + c), dsem.at[8], up)
    arrived(rel.at[1], dsem.at[1])
    send(rel.at[1], dyslot(1, yp * 2 + c), dsem.at[9], down)
    arrived(xg.at[g_pa], tsem.at[2])
    xsend(0)
    xsend(1)
    arrived(xh_p, tsem.at[1])
    arrived(dyh_p, tsem.at[0])
    hmultiply()
    hstart()
    gd, gu, gf = ym * 2 + c, yp * 2 + c, y2 * 2 + c
    for n, (g, j, s) in enumerate(((gd, 0, 2), (gu, 0, 4), (gd, 1, 3), (gu, 1, 5))):
        arrived(dyslot(j, g), dsem.at[s])
        send(dyslot(j, g), dyslot(j, g), dsem.at[10 + n], partner)
    hstep(3)
    for n, (g, j, s) in enumerate(((gf, 0, 8), (gf, 1, 9))):
        arrived(dyslot(j, g), dsem.at[s])
        send(dyslot(j, g), dyslot(j, g), dsem.at[14 + n], partner)
    xforward(0)
    pd, pu, pf = ym * 2 + 1 - c, yp * 2 + 1 - c, y2 * 2 + 1 - c
    for g, j, s in ((g_pa, 0, 6), (g_pa, 1, 7), (pd, 0, 10), (pu, 0, 11), (pd, 1, 12), (pu, 1, 13), (pf, 0, 14), (pf, 1, 15)):
        arrived(dyslot(j, g), dsem.at[s])

    for k in range(NZ):
        if k + 2 < NZ:
            xsend(k + 2)
        if k + 1 < NZ:
            xforward(k + 1)
        zk = zof(k)
        arrived(xg.at[y2 * 2 + c, zk], xsem.at[k * 6 + 4])
        arrived(xg.at[y2 * 2 + 1 - c, zk], xsem.at[k * 6 + 5])
        compute(k)
        if k >= 1:
            xsum(k - 1)
        if k >= 2:
            zsum(k - 2)
        if k == 0:
            hstep(2)
        elif k == 2:
            hstep(1)
        elif k == 3:
            hlast()
        elif k == 4:
            hx()
        elif k == 5:
            hxlast()
        elif k == 6:
            hyadd()
    xsum(NZ - 1)
    zsum(NZ - 2)
    hylast()
    zsum(NZ - 1)
    for op in started:
        op.wait_send()


def shards(x_rows, dy_rows, seg_blocks):
    dp, ex = lax.axis_index("dp"), lax.axis_index("expert")
    bf16, f32, i16 = jnp.bfloat16, jnp.float32, jnp.int16
    i32 = jnp.int32
    hot = jnp.argmax(jnp.all(seg_blocks == 2, axis=0)).astype(i32)
    g = jnp.arange(NG, dtype=i32)
    devices = ((dp // 2) * 2 + g % 2) * NG + (ex // NY) * NY + g // 2
    counts = seg_blocks[devices]
    ends = jnp.cumsum(counts, axis=1)
    first = jnp.sum(jnp.where(jnp.arange(NE)[None, :] < hot, counts, 0), axis=1)
    slot = jnp.arange(2, dtype=i32)[None, :]
    cold = jnp.where(slot < first[:, None], slot, slot + 2)
    owner = jnp.sum((ends[:, None, :] <= cold[:, :, None]).astype(i32), axis=2)
    r = jnp.arange(NC, dtype=i32)
    names = r + (r >= hot).astype(i32)
    mask = jnp.repeat((owner[:, None, :] == names[None, :, None]).astype(bf16), BLOCK, axis=2)
    mask = mask.reshape(NG // GG, GG, NC, TOK).transpose(0, 2, 1, 3).reshape(NG // GG, NC, GG * TOK)
    me = (ex % NY) * 2 + dp % 2
    low = slot[0] < first[me]
    pos = jnp.broadcast_to(jnp.stack([low, ~low], axis=1).reshape(4, 1).astype(bf16), (4, 8 * FC))
    vm = pl.BlockSpec(memory_space=pltpu.VMEM)
    sem = pltpu.SemaphoreType.DMA
    res = pl.pallas_call(
        kernel,
        out_shape=jax.ShapeDtypeStruct((NE, HR, FC), f32),
        in_specs=[vm] * 4,
        out_specs=vm,
        scratch_shapes=[
            pltpu.VMEM((2, NZ, 2, HR, TOK), bf16),
            pltpu.VMEM((2, NZ, 2, HR, TOK), bf16),
            pltpu.VMEM((NZ, 2, HR, TOK), bf16),
            pltpu.VMEM((NG, NZ, 2, HR, TOK), bf16),
            pltpu.VMEM((TOK, 8 * FC), bf16),
            pltpu.VMEM((TOK, 8 * FC), bf16),
            pltpu.VMEM((TOK, 8 * FC), bf16),
            pltpu.VMEM((2, NG * TOK, FC), bf16),
            pltpu.VMEM((2, TOK, FC), bf16),
            pltpu.VMEM((2 * NC * HR, GG * TOK), bf16),
            pltpu.VMEM((3, 2, 2, NC * HR, FC), f32),
            pltpu.VMEM((8, NZ, 2, HR, FC), f32),
            pltpu.VMEM((NZ, 2, MSG, FC), i16),
            pltpu.VMEM((NZ, 2, MSG, FC), i16),
            pltpu.VMEM((NZ, 2, 2, MSG, FC), i16),
            pltpu.VMEM((NZ, 2, 2, MSG, FC), i16),
            pltpu.VMEM((NZ, 2, MSG, FC), i16),
            pltpu.VMEM((NZ, 2, 2, MSG, FC), i16),
            pltpu.VMEM((NZ, 4, MSG, FC), i16),
            pltpu.VMEM((NZ, 2, 4, MSG, FC), i16),
            pltpu.VMEM((4, 4, HR, FC), f32),
            pltpu.VMEM((2, MSG, FC), i16),
            pltpu.VMEM((2, MSG, FC), i16),
            pltpu.VMEM((2, MSG, FC), i16),
            pltpu.VMEM((2, MSG, FC), i16),
            pltpu.VMEM((4, HR, FC), f32),
            pltpu.VMEM((HR, FC), f32),
            pltpu.VMEM((3, HR, FC), f32),
            pltpu.VMEM((16, FC), f32),
            sem((16, 2)), sem((48, 2)), sem((16, 2)), sem((32, 2)), sem((32, 2)), sem((64, 2)), sem((10, 2)),
        ],
        compiler_params=pltpu.CompilerParams(
            collective_id=0, has_side_effects=True, vmem_limit_bytes=58 << 20),
    )(pos, x_rows, dy_rows, mask)
    e = jnp.arange(NE, dtype=i32)
    return res[jnp.where(e == hot, 0, 1 + e - (e > hot).astype(i32))]


def solution(mesh):
    in_specs = (P(("dp", "expert"), None), P(("dp", "expert"), None), P())
    out_specs = P(None, "dp", "expert")
    return jax.shard_map(shards, mesh=mesh, in_specs=in_specs, out_specs=out_specs, check_vma=False)
```

time: 319 us -> 89.9 us (0.28)
  waiting for transfers between devices: 260 us -> 0 us
  Pallas kernels: 0 us -> 78.8 us
  matrix products: 22.7 us -> 0 us
  between operations: 13.4 us -> 0.09 us
  local copies, waits for them, and re-layouts: 15.8 us -> 5.81 us
  starting transfers between devices: 5.85 us -> 0 us
  other arithmetic: 0.39 us -> 5.02 us
    reduce_scatter x1 -> x0, waiting for transfers between devices: 158 us -> none  [shards(): return lax.psum_scatter(part, 'dp', scatter_dimension=1, tiled=True)]
    all_gather x1 -> x0, waiting for transfers between devices: 102 us -> none  [shards(): xg = lax.all_gather(x_rows, 'expert', axis=0, tiled=True)]
    pallas_call x0 -> x1, Pallas kernels: none -> 78.8 us  [shards(): pl.pallas_call(kernel, out_shape=jax.ShapeDtypeStruct((NE, HR, FC), f32),...]
    dot_general x1 -> x0, matrix products: 22.7 us -> none  [shards(): jnp.einsum('eth,tf->ehf', xm, dyg, preferred_element_type=jnp.float32)]
    all_gather x1 -> x0, local copies, waits for them, and re-layouts: 11.8 us -> none  [shards(): xg = lax.all_gather(x_rows, 'expert', axis=0, tiled=True)]
    all_to_all x1 -> x0, starting transfers between devices: 5.84 us -> none  [shards(): lax.all_to_all(dy_rows, 'expert', split_axis=1, concat_axis=0, tiled=True)]
  transfers between devices with their start and end apart: 3 -> 0, of which waited for: 2 -> 0; matrix products, arithmetic and copies ran while one was open for 5% -> 0% of each run, Pallas kernels for 0% -> 0%
where the time goes in v3:
time: 89.9 us; the launch traced here: 89.7 us
  Pallas kernels  78.8 us (88%)
  local copies, waits for them, and re-layouts  5.81 us (6%)
  other arithmetic  5.02 us (6%)
    pallas_call x1, Pallas kernels, shards(): pl.pallas_call(kernel, out_shape=jax.ShapeDtypeStruct((NE, HR, FC), f32),...  78.8 us
    gather x1, local copies, waits for them, and re-layouts, shards(): return res[jnp.where(e == hot, 0, 1 + e - (e > hot).astype(i32))]  2.21 us

profile of v3, /device:TPU:8, one launch (start us, length us, event | category | flops | bytes accessed | tf_op | source)
XLA Modules:
  0.0 89.7 jit_solution(2743203521087428439)
XLA Ops:
  0.0 0.8 compare_reduce_fusion
  0.8 0.7 iota_reduce_fusion
  1.6 0.7 fusion.7
  2.3 0.7 fusion.4
  3.0 0.7 iota_compare_fusion.1
  3.7 0.8 copy.7
  4.5 0.6 gather_fusion
  5.1 0.1 select_reduce_fusion
  5.2 0.6 dynamic_slice.3
  5.8 0.1 compare_select_fusion.3
  5.9 0.2 reduce_window_sum.11
  6.0 0.2 convert_reduce_fusion
  6.2 0.7 iota_compare_fusion
  6.9 0.1 add_convert_fusion
  7.0 0.1 reshape.192
  7.1 0.1 copy.8
  7.1 0.1 compare_convert_fusion
  7.2 0.1 broadcast_in_dim.49
  7.4 0.6 copy.9.msk
  8.0 0.7 broadcast_in_dim.34.pos
  8.7 78.8 %shard_map.37 = f32[8,32,256]{2,1,0:T(8,128)} custom-call(bf16[4,2048]{1,0:T(4,128)(2,1)} %broadcast_in_dim.34.pos, bf16[512,1024]{1,0:T(8,128)(2,1)} %x.1, bf16[512,2048]{1,0:T(8,128)(2,1)} %dy.1, bf16[2,7,1024]{2,1,0:T(8,128)(2,1)} %copy.9.msk), custom_call_target="tpu_custom_call" | custom-call | tf_op jit(solution)/shard_map/pallas_call | solution.py:348
  87.5 2.2 %gather_fusion.1 = f32[8,32,256]{2,1,0:T(8,128)} fusion(f32[8,32,256]{2,1,0:T(8,128)} %shard_map.37, s32[1024]{0:T(1024)S(1)} %pad_clamp_fusion), kind=kCustom, calls=%fused_computation.1 | custom fusion | bytes 524320 | tf_op jit(solution)/shard_map/gather | solution.py:389
  (6 shorter events, 0.1 us)

commit v4 on v3

--- a/solution.py
+++ b/solution.py
@@ -10,7 +10,8 @@
 BLOCK = 128
 NE = 8
 NC = NE - 1
-NB = (4, 3)
+NX1 = 5
+NB = (3, 2)
 TOK = 2 * BLOCK
 NY, NX, NZ = 4, 4, 8
 NG = 2 * NY
@@ -50,9 +51,13 @@
     return pl.ds(0, n * HR + 16)
 
 
-def kernel(pos, x, dy, msk, out, xo_h, xo_c, xh_p, xg, dyh_o, dyh_p, dyc, dyg, rel, lhs, part, hp, xa_s, xa_r, xb_s, xb_r,
+def flag(cond):
+    return jnp.where(cond, 1.0, 0.0).astype(jnp.float32)
+
+
+def kernel(seg, segv, x_any, dy_any, out, x, dy, msk, xo_h, xo_c, xh_p, xg, dyh_o, dyh_p, dyc, dyg, rel, lhs, part, hp, xa_s, xa_r, xb_s, xb_r,
            z_s, z_r, hz_s, hz_r, hr, hxa_s, hxa_r, hxb_s, hxb_r, hy, hy_s, hy_r, scales,
-           dsem, xsem, asem, bsem, zsem, hsem, tsem):
+           cz_s, cz_r, cr, cxa_r, cx_s, cxb_r, res, dsem, xsem, asem, bsem, zsem, hsem, tsem, csem, cxsem, lsem):
     dp, ex = lax.axis_index("dp"), lax.axis_index("expert")
     z, xh, c = dp // 4, (dp // 2) % 2, dp % 2
     xl, y = ex // NY, ex % NY
@@ -73,16 +78,53 @@
     barrier = pltpu.get_barrier_semaphore()
     for other in (partner, up, down, right, left, ahead, behind):
         pl.semaphore_signal(barrier, inc=1, device_id=other, device_id_type=pl.DeviceIdType.MESH)
+    load_dy = pltpu.make_async_copy(dy_any, dy, lsem.at[0])
+    load_x = pltpu.make_async_copy(x_any, x, lsem.at[1])
+    load_dy.start()
+    load_x.start()
     scales[...] = jnp.zeros_like(scales)
 
-    def pick(ref, j, i, n):
+    twos = jnp.min(jnp.where(segv[...] == 2, 1.0, 0.0), axis=1, keepdims=True)
+    index = lax.broadcasted_iota(jnp.int32, (NE, 1), 0)
+    hot = jnp.min(jnp.where(twos > 0.5, index, NE))
+
+    def cold_blocks(g):
+        device = ((dp // 2) * 2 + g % 2) * NG + xl * NY + g // 2
+        ends, first, total = [], 0, 0
+        for e in range(NE):
+            n = seg[e, device]
+            total = total + n
+            ends.append(total)
+            first = first + jnp.where(e < hot, n, 0)
+        picked = []
+        for j in range(2):
+            low = j < first
+            at_ = jnp.where(low, j, j + 2)
+            owner = 0
+            for e in range(NE):
+                owner = owner + jnp.where(ends[e] <= at_, 1, 0)
+            picked.append((low, owner))
+        return picked
+
+    for g in range(NG):
+        for j, (_, owner) in enumerate(cold_blocks(g)):
+            for e in range(NC):
+                name = e + jnp.where(e >= hot, 1, 0)
+                lanes = slice((g % GG) * TOK + j * BLOCK, (g % GG) * TOK + (j + 1) * BLOCK)
+                msk[g // GG, e:e + 1, lanes] = jnp.full((1, BLOCK), flag(owner == name), jnp.float32)
+    low = [flag(c_[0]) for c_ in cold_blocks(g_me)]
+
+    def pick(ref, j, i, n, width):
+        w = low[j] if i == 1 else 1.0 - low[j]
         a, b = ref[j * BLOCK:(j + 1) * BLOCK, n], ref[(j + 2) * BLOCK:(j + 3) * BLOCK, n]
-        m = 2 * j + 1 - i
-        return a * pos[m:m + 1, n] + b * pos[2 * j + i:2 * j + i + 1, n]
-
+        return (a * jnp.full((1, width), w, jnp.float32).astype(a.dtype)
+                + b * jnp.full((1, width), 1.0 - w, jnp.float32).astype(b.dtype))
+
+    load_dy.wait()
     for i, dst in ((1, dyc), (0, dyh_o)):
         for j in range(2):
-            dst[j * BLOCK:(j + 1) * BLOCK, :] = pick(dy, j, i, slice(0, 8 * FC))
+            dst[j * BLOCK:(j + 1) * BLOCK, :] = pick(dy, j, i, slice(0, 8 * FC), 8 * FC)
+    load_x.wait()
     pl.semaphore_wait(barrier, 7)
 
     started = []
@@ -118,7 +160,7 @@
 
     def turn(n, _):
         for j in range(4):
-            t = pick(x, j % 2, j // 2, pl.ds(pl.multiple_of(n * BLOCK, BLOCK), BLOCK)).T
+            t = pick(x, j % 2, j // 2, pl.ds(pl.multiple_of(n * BLOCK, BLOCK), BLOCK), BLOCK).T
             dst = (xo_h, xo_c)[j // 2]
             for i in range(4):
                 dst[i % 2, n, i // 2, :, (j % 2) * BLOCK:(j % 2 + 1) * BLOCK] = t[i * HR:(i + 1) * HR, :]
@@ -212,7 +254,7 @@
     def hylast():
         arrived(hy_r.at[2], tsem.at[8])
         arrived(hy_r.at[1], tsem.at[9])
-        out[0] = hy[y] + hy_r[1] + hy_r[2]
+        res[0] = hy[y] + hy_r[1] + hy_r[2]
 
     def multiply(k):
         b, zk = k % 3, zof(k)
@@ -220,14 +262,14 @@
             for h in range(2):
                 v = jnp.concatenate([xg[q * GG + i, zk, h] for i in range(GG)], axis=1)
                 for e in range(NC):
-                    lhs[(h * NC + e) * HR:(h * NC + e + 1) * HR, :] = v * msk[q, e:e + 1, :]
+                    lhs[(h * NC + e) * HR:(h * NC + e + 1) * HR, :] = v * msk[q, e:e + 1, :].astype(v.dtype)
             for j in range(2):
                 r = jnp.dot(lhs[...], dyg[j, q * GG * TOK:(q + 1) * GG * TOK, :], preferred_element_type=jnp.float32)
                 r = r.reshape(2, NC * HR, FC)
                 part[b, j] = r if q == 0 else part[b, j] + r
 
     def rows(k, x_, h):
-        return lambda e: part[k % 3, x_ % 2, x_ // 2, (h * 4 + e) * HR:(h * 4 + e + 1) * HR, :]
+        return lambda e: part[k % 3, x_ % 2, x_ // 2, (h * NB[0] + e) * HR:(h * NB[0] + e + 1) * HR, :]
 
     def compute(k):
         multiply(k)
@@ -259,13 +301,57 @@
             get = plus(*terms)
             if off == 0:
                 for e in range(n):
-                    out[1 + h * 4 + e] = get(e)
+                    res[1 + h * NB[0] + e] = get(e)
                 continue
             encode(z_s.at[k, h], scales, n, get)
             i = h if off == 4 else (0 if off > 0 else 1)
             m = OFFS.index((3, -3)[i] if off == 4 else (off - 1 if off > 0 else off + 1))
             send(z_s.at[k, h, span(n)], z_r.at[m, i, h, span(n)], zsem.at[(m * 2 + i) * 2 + h], (ahead, behind)[i])
 
+    def czrows(k, u):
+        return lambda i: part[k % 3, i // 2, u, (NX1 + i % 2) * HR:(NX1 + i % 2 + 1) * HR, :]
+
+    def czsum(k):
+        off = OFFS[k]
+        for u in range(2):
+            terms = [czrows(k, u)]
+            for i in range(2):
+                sign = off if i == 0 else -off
+                if sign in (0, 1, 2) or (sign == 3 and u == i):
+                    arrived(cz_r.at[k, i, u], csem.at[(k * 2 + i) * 2 + u])
+                    terms.append(decoder(cz_r.at[k, i, u], 4))
+            get = plus(*terms)
+            if off == 0:
+                for i in range(4):
+                    cr[u * 2 + i // 2, i % 2] = get(i)
+                continue
+            encode(cz_s.at[k, u], scales, 4, get)
+            i = u if off == 4 else (0 if off > 0 else 1)
+            m = OFFS.index((3, -3)[i] if off == 4 else (off - 1 if off > 0 else off + 1))
+            send(cz_s.at[k, u], cz_r.at[m, i, u], csem.at[(m * 2 + i) * 2 + u], (ahead, behind)[i])
+
+    def cxsend():
+        for i, x_, dev in ((0, xp, right), (1, xm, left)):
+            send(cr.at[x2, i], cxa_r.at[i], cxsem.at[i], dev)
+            send(cr.at[x_, 1 - i], cxb_r.at[i, 1 - i], cxsem.at[2 + i * 2 + 1 - i], dev)
+
+    def cxsum():
+        for i, x_, dev in ((0, xp, right), (1, xm, left)):
+            arrived(cxa_r.at[i], cxsem.at[i])
+            cx_s[i] = cr[x_, i] + cxa_r[i]
+            send(cx_s.at[i], cxb_r.at[i, i], cxsem.at[2 + i * 2 + i], dev)
+
+    def cxlast():
+        for i in range(2):
+            for e in range(2):
+                arrived(cxb_r.at[i, e], cxsem.at[2 + i * 2 + e])
+        for e in range(2):
+            res[1 + NX1 + e] = cr[X, e] + cxb_r[0, e] + cxb_r[1, e]
+
+    arrived(xh_p, tsem.at[1])
+    arrived(dyh_p, tsem.at[0])
+    hmultiply()
+    hstart()
     arrived(rel.at[0], dsem.at[0])
     send(rel.at[0], dyslot(0, ym * 2 + c), dsem.at[8], up)
     arrived(rel.at[1], dsem.at[1])
@@ -273,18 +359,14 @@
     arrived(xg.at[g_pa], tsem.at[2])
     xsend(0)
     xsend(1)
-    arrived(xh_p, tsem.at[1])
-    arrived(dyh_p, tsem.at[0])
-    hmultiply()
-    hstart()
     gd, gu, gf = ym * 2 + c, yp * 2 + c, y2 * 2 + c
     for n, (g, j, s) in enumerate(((gd, 0, 2), (gu, 0, 4), (gd, 1, 3), (gu, 1, 5))):
         arrived(dyslot(j, g), dsem.at[s])
         send(dyslot(j, g), dyslot(j, g), dsem.at[10 + n], partner)
-    hstep(3)
     for n, (g, j, s) in enumerate(((gf, 0, 8), (gf, 1, 9))):
         arrived(dyslot(j, g), dsem.at[s])
         send(dyslot(j, g), dyslot(j, g), dsem.at[14 + n], partner)
+    hstep(3)
     xforward(0)
     pd, pu, pf = ym * 2 + 1 - c, yp * 2 + 1 - c, y2 * 2 + 1 - c
     for g, j, s in ((g_pa, 0, 6), (g_pa, 1, 7), (pd, 0, 10), (pu, 0, 11), (pd, 1, 12), (pu, 1, 13), (pf, 0, 14), (pf, 1, 15)):
@@ -299,6 +381,9 @@
         arrived(xg.at[y2 * 2 + c, zk], xsem.at[k * 6 + 4])
         arrived(xg.at[y2 * 2 + 1 - c, zk], xsem.at[k * 6 + 5])
         compute(k)
+        czsum(k)
+        if k == NZ - 1:
+            cxsend()
         if k >= 1:
             xsum(k - 1)
         if k >= 2:
@@ -315,42 +400,36 @@
             hxlast()
         elif k == 6:
             hyadd()
+    cxsum()
     xsum(NZ - 1)
     zsum(NZ - 2)
     hylast()
+    cxlast()
     zsum(NZ - 1)
+    for e in range(NE):
+        v = res[0] * flag(e == hot)
+        if e < NC:
+            v = v + res[1 + e] * flag(e < hot)
+        if e > 0:
+            v = v + res[e] * flag(e > hot)
+        out[e] = v
     for op in started:
         op.wait_send()
 
 
 def shards(x_rows, dy_rows, seg_blocks):
-    dp, ex = lax.axis_index("dp"), lax.axis_index("expert")
     bf16, f32, i16 = jnp.bfloat16, jnp.float32, jnp.int16
-    i32 = jnp.int32
-    hot = jnp.argmax(jnp.all(seg_blocks == 2, axis=0)).astype(i32)
-    g = jnp.arange(NG, dtype=i32)
-    devices = ((dp // 2) * 2 + g % 2) * NG + (ex // NY) * NY + g // 2
-    counts = seg_blocks[devices]
-    ends = jnp.cumsum(counts, axis=1)
-    first = jnp.sum(jnp.where(jnp.arange(NE)[None, :] < hot, counts, 0), axis=1)
-    slot = jnp.arange(2, dtype=i32)[None, :]
-    cold = jnp.where(slot < first[:, None], slot, slot + 2)
-    owner = jnp.sum((ends[:, None, :] <= cold[:, :, None]).astype(i32), axis=2)
-    r = jnp.arange(NC, dtype=i32)
-    names = r + (r >= hot).astype(i32)
-    mask = jnp.repeat((owner[:, None, :] == names[None, :, None]).astype(bf16), BLOCK, axis=2)
-    mask = mask.reshape(NG // GG, GG, NC, TOK).transpose(0, 2, 1, 3).reshape(NG // GG, NC, GG * TOK)
-    me = (ex % NY) * 2 + dp % 2
-    low = slot[0] < first[me]
-    pos = jnp.broadcast_to(jnp.stack([low, ~low], axis=1).reshape(4, 1).astype(bf16), (4, 8 * FC))
     vm = pl.BlockSpec(memory_space=pltpu.VMEM)
     sem = pltpu.SemaphoreType.DMA
-    res = pl.pallas_call(
+    return pl.pallas_call(
         kernel,
         out_shape=jax.ShapeDtypeStruct((NE, HR, FC), f32),
-        in_specs=[vm] * 4,
+        in_specs=[pl.BlockSpec(memory_space=pltpu.SMEM), vm] + [pl.BlockSpec(memory_space=pl.ANY)] * 2,
         out_specs=vm,
         scratch_shapes=[
+            pltpu.VMEM(x_rows.shape, bf16),
+            pltpu.VMEM(dy_rows.shape, bf16),
+            pltpu.VMEM((NG // GG, NE, GG * TOK), f32),
             pltpu.VMEM((2, NZ, 2, HR, TOK), bf16),
             pltpu.VMEM((2, NZ, 2, HR, TOK), bf16),
             pltpu.VMEM((NZ, 2, HR, TOK), bf16),
@@ -380,13 +459,19 @@
             pltpu.VMEM((HR, FC), f32),
             pltpu.VMEM((3, HR, FC), f32),
             pltpu.VMEM((16, FC), f32),
+            pltpu.VMEM((NZ, 2, MSG, FC), i16),
+            pltpu.VMEM((NZ, 2, 2, MSG, FC), i16),
+            pltpu.VMEM((4, 2, HR, FC), f32),
+            pltpu.VMEM((2, HR, FC), f32),
+            pltpu.VMEM((2, HR, FC), f32),
+            pltpu.VMEM((2, 2, HR, FC), f32),
+            pltpu.VMEM((NE, HR, FC), f32),
             sem((16, 2)), sem((48, 2)), sem((16, 2)), sem((32, 2)), sem((32, 2)), sem((64, 2)), sem((10, 2)),
+            sem((32, 2)), sem((6, 2)), sem((2,)),
         ],
         compiler_params=pltpu.CompilerParams(
             collective_id=0, has_side_effects=True, vmem_limit_bytes=58 << 20),
-    )(pos, x_rows, dy_rows, mask)
-    e = jnp.arange(NE, dtype=i32)
-    return res[jnp.where(e == hot, 0, 1 + e - (e > hot).astype(i32))]
+    )(seg_blocks.T, seg_blocks.T, x_rows, dy_rows)
 
 
 def solution(mesh):

time: 89.9 us -> 80.9 us (0.90)
  other arithmetic: 5.02 us -> 0 us
  local copies, waits for them, and re-layouts: 5.81 us -> 1.67 us
    gather x2 -> x0, local copies, waits for them, and re-layouts: 2.77 us -> none  [the longest x1 2.21 us: shards(): return res[jnp.where(e == hot, 0, 1 + e - (e > hot).astype(i32))]]
    lt x2 -> x0, other arithmetic: 1.35 us -> none  [the longest x1 0.69 us: shards(): first = jnp.sum(jnp.where(jnp.arange(NE)[None, :] < hot, counts, 0), axis=1)]
where the time goes in v4:
time: 80.9 us; the launch traced here: 80.4 us
  Pallas kernels  78.7 us (97%)
  local copies, waits for them, and re-layouts  1.67 us (2%)
    pallas_call x1, Pallas kernels, shards(): pl.pallas_call(kernel, out_shape=jax.ShapeDtypeStruct((NE, HR, FC), f32),...  78.7 us
    unnamed x1, local copies, waits for them, and re-layouts  1.67 us

profile of v4, /device:TPU:8, one launch (start us, length us, event | category | flops | bytes accessed | tf_op | source)
XLA Modules:
  0.0 80.4 jit_solution(3582611898967482870)
XLA Ops:
  0.0 78.7 %shard_map.37 = f32[8,32,256]{2,1,0:T(8,128)} custom-call(s32[8,256]{1,0:T(8,128)} %bitcast.1, s32[8,256]{1,0:T(8,128)} %bitcast.2, bf16[512,1024]{1,0:T(8,128)(2,1)} %x_any.1, bf16[512,2048]{1,0:T(8,128)(2,1)} %dy_any.1), custom_call_target="tpu_custom_call" | custom-call | tf_op jit(solution)/shard_map/pallas_call | solution.py:424
  78.7 1.7 %copy.5 = f32[8,32,256]{2,1,0:T(8,128)} copy(f32[8,32,256]{2,1,0:T(8,128)} %shard_map.37) | data formatting | bytes 524288

commit v5 on v4

--- a/solution.py
+++ b/solution.py
@@ -55,9 +55,24 @@
     return jnp.where(cond, 1.0, 0.0).astype(jnp.float32)
 
 
-def kernel(seg, segv, x_any, dy_any, out, x, dy, msk, xo_h, xo_c, xh_p, xg, dyh_o, dyh_p, dyc, dyg, rel, lhs, part, hp, xa_s, xa_r, xb_s, xb_r,
-           z_s, z_r, hz_s, hz_r, hr, hxa_s, hxa_r, hxb_s, hxb_r, hy, hy_s, hy_r, scales,
-           cz_s, cz_r, cr, cxa_r, cx_s, cxb_r, res, dsem, xsem, asem, bsem, zsem, hsem, tsem, csem, cxsem, lsem):
+def hops():
+    found = {}
+    for k, off in enumerate(OFFS):
+        for i in range(2):
+            for u in range(2):
+                sign = off if i == 0 else -off
+                if sign in (0, 1, 2) or (sign == 3 and u == i):
+                    found[k, i, u] = len(found)
+    return found
+
+
+HOPS = hops()
+
+
+def kernel(seg, segv, x_any, dy_any, out, x, dy, msk, xo_h, xo_c, xh_p, xg, dyh_o, dyh_p, dyc, dyg, rel, lhs, part, hp,
+           xa_s, xa_r, xb_s, xb_r, z_s, z_r, cz_s, cz_r, cr, cxa_r, cx_s, cxb_r, hz_s, hz_r, hr, ha_r, hs_s, hb_r,
+           ga_s, ga_r, gb_s, gb_r, hq, hq_s, hq_r, hy, hy_s, hy_r, scales, res,
+           dsem, xsem, asem, bsem, zsem, csem, cxsem, hsem, hxsem, gsem, qsem, tsem, lsem):
     dp, ex = lax.axis_index("dp"), lax.axis_index("expert")
     z, xh, c = dp // 4, (dp // 2) % 2, dp % 2
     xl, y = ex // NY, ex % NY
@@ -194,70 +209,116 @@
             r = jnp.concatenate([dyh_o[:, n * FC:(n + 1) * FC], dyh_p[:, n * FC:(n + 1) * FC]], axis=0)
             hp[n] = jnp.dot(left_, r, preferred_element_type=jnp.float32).reshape(NZ, 2, HR, FC)
 
+    def over_z(rows_of, n, s_, r_, sem, last):
+        def step(k):
+            off = OFFS[k]
+            for u in range(2):
+                terms = [rows_of(k, u)]
+                for i in range(2):
+                    if (k, i, u) in HOPS:
+                        m = HOPS[k, i, u]
+                        arrived(r_.at[m], sem.at[m])
+                        terms.append(decoder(r_.at[m], n) if n > 1 else lambda e, m=m: r_[m])
+                get = plus(*terms)
+                if off == 0:
+                    for e in range(n):
+                        last(u, e, get(e))
+                    continue
+                i = u if off == 4 else (0 if off > 0 else 1)
+                m = HOPS[OFFS.index((3, -3)[i] if off == 4 else (off - 1 if off > 0 else off + 1)), i, u]
+                if n > 1:
+                    encode(s_.at[k, u], scales, n, get)
+                else:
+                    s_[k, u] = get(0)
+                send(s_.at[k, u], r_.at[m], sem.at[m], (ahead, behind)[i])
+        return step
+
+    def over_x(acc, a_r, s_, b_r, sem):
+        way = ((0, xp, right), (1, xm, left))
+
+        def begin():
+            for i, x_, dev in way:
+                send(acc.at[x2, i], a_r.at[i], sem.at[i], dev)
+                send(acc.at[x_, 1 - i], b_r.at[i, 1 - i], sem.at[2 + i * 2 + 1 - i], dev)
+
+        def middle():
+            for i, x_, dev in way:
+                arrived(a_r.at[i], sem.at[i])
+                s_[i] = acc[x_, i] + a_r[i]
+                send(s_.at[i], b_r.at[i, i], sem.at[2 + i * 2 + i], dev)
+
+        def end(put):
+            for i in range(2):
+                for e in range(2):
+                    arrived(b_r.at[i, e], sem.at[2 + i * 2 + e])
+            for e in range(2):
+                put(e, acc[X, e] + b_r[0, e] + b_r[1, e])
+        return begin, middle, end
+
     def hrows(k, u):
         zk = zof(k)
-        return lambda i: hp[(u % 2) * NY + i, zk, u // 2]
-
-    def hstart():
-        for u, n, i, dev in ((0, 1, 0, ahead), (2, 2, 1, behind), (1, 1, 0, ahead), (3, 2, 1, behind)):
-            encode(hz_s.at[0, u], scales, 4, hrows(0, u))
-            send(hz_s.at[0, u], hz_r.at[n, i, u], hsem.at[(n * 2 + i) * 4 + u], dev)
-
-    def hstep(off):
+        return lambda i: hp[(i // 2) * NY + 2 + i % 2, zk, u]
+
+    def hput(u, i, v):
+        hr[u * 2 + i // 2, i % 2] = v
+
+    def hyput(e, v):
+        hy[2 + e] = v
+
+    hz = over_z(hrows, 4, hz_s, hz_r, hsem, hput)
+    hx_begin, hx_middle, hx_end = over_x(hr, ha_r, hs_s, hb_r, hxsem)
+
+    def grows(x_, t):
+        return lambda i: hp[(x_ % 2) * NY + i % 2, 2 * t + i // 2, x_ // 2]
+
+    def gsend(src, rcv, sem, dev, get):
+        encode(src, scales, 4, get)
+        send(src, rcv, sem, dev)
+
+    def gx_begin():
+        for t, dev in ((0, right), (2, left), (1, right), (3, left)):
+            gsend(ga_s.at[t], ga_r.at[t], gsem.at[t], dev, grows(x2, t))
+        for i, t, x_, dev in ((0, 2, xp, right), (1, 0, xm, left), (0, 3, xp, right), (1, 1, xm, left)):
+            gsend(gb_s.at[i, t], gb_r.at[i, t], gsem.at[4 + i * 4 + t], dev, grows(x_, t))
+
+    def gx_middle():
+        for i, t, x_, dev in ((0, 0, xp, right), (1, 2, xm, left), (0, 1, xp, right), (1, 3, xm, left)):
+            arrived(ga_r.at[t], gsem.at[t])
+            gsend(gb_s.at[i, t], gb_r.at[i, t], gsem.at[4 + i * 4 + t], dev, plus(grows(x_, t), decoder(ga_r.at[t], 4)))
+
+    def gx_end():
         for t in range(4):
-            for i, dev in ((0, ahead), (1, behind)):
-                k = OFFS.index(off if i == 0 else -off)
-                n = OFFS.index(off - 1 if i == 0 else 1 - off)
-                u = ((2, 3, 0, 1) if i == 0 else (0, 1, 2, 3))[t]
-                get = hrows(k, u)
-                if off < 3 or t >= 2:
-                    arrived(hz_r.at[k, i, u], hsem.at[(k * 2 + i) * 4 + u])
-                    get = plus(get, decoder(hz_r.at[k, i, u], 4))
-                encode(hz_s.at[k, u], scales, 4, get)
-                send(hz_s.at[k, u], hz_r.at[n, i, u], hsem.at[(n * 2 + i) * 4 + u], dev)
-
-    def hlast():
-        for u in range(4):
             for i in range(2):
-                arrived(hz_r.at[7, i, u], hsem.at[(7 * 2 + i) * 4 + u])
-            get = plus(hrows(7, u), decoder(hz_r.at[7, 0, u], 4), decoder(hz_r.at[7, 1, u], 4))
+                arrived(gb_r.at[i, t], gsem.at[4 + i * 4 + t])
+            get = plus(grows(X, t), decoder(gb_r.at[0, t], 4), decoder(gb_r.at[1, t], 4))
             for i in range(4):
-                hr[u, i] = get(i)
-        encode(hxa_s.at[0], scales, 2, lambda i: hr[x2, i])
-        send(hxa_s.at[0, span(2)], hxa_r.at[0, span(2)], tsem.at[3], right)
-        encode(hxa_s.at[1], scales, 2, lambda i: hr[x2, 2 + i])
-        send(hxa_s.at[1, span(2)], hxa_r.at[1, span(2)], tsem.at[4], left)
-
-    def hx():
-        arrived(hxa_r.at[0, span(2)], tsem.at[3])
-        arrived(hxa_r.at[1, span(2)], tsem.at[4])
-        d0, d1 = decoder(hxa_r.at[0], 2), decoder(hxa_r.at[1], 2)
-        encode(hxb_s.at[0], scales, 4, lambda i: hr[xp, i] + d0(i) if i < 2 else hr[xp, i])
-        send(hxb_s.at[0], hxb_r.at[0], tsem.at[5], right)
-        encode(hxb_s.at[1], scales, 4, lambda i: hr[xm, i] + d1(i - 2) if i >= 2 else hr[xm, i])
-        send(hxb_s.at[1], hxb_r.at[1], tsem.at[6], left)
-
-    def hxlast():
-        arrived(hxb_r.at[0], tsem.at[5])
-        arrived(hxb_r.at[1], tsem.at[6])
-        get = plus(lambda i: hr[X, i], decoder(hxb_r.at[0], 4), decoder(hxb_r.at[1], 4))
-        for i in range(4):
-            hy[i] = get(i)
-        send(hy.at[y2], hy_r.at[0], tsem.at[7], up)
-        send(hy.at[ym], hy_r.at[2], tsem.at[8], down)
-
-    def hyadd():
-        arrived(hy_r.at[0], tsem.at[7])
+                hq[i % 2, 2 * t + i // 2] = get(i)
+
+    def qrows(k, u):
+        zk = zof(k)
+        return lambda e: hq[u, zk]
+
+    def qput(u, e, v):
+        hy[u] = v
+
+    gz = over_z(qrows, 1, hq_s, hq_r, qsem, qput)
+
+    def hy_begin():
+        send(hy.at[y2], hy_r.at[0], tsem.at[3], up)
+        send(hy.at[ym], hy_r.at[2], tsem.at[4], down)
+
+    def hy_middle():
+        arrived(hy_r.at[0], tsem.at[3])
         hy_s[...] = hy[yp] + hy_r[0]
-        send(hy_s, hy_r.at[1], tsem.at[9], up)
-
-    def hylast():
-        arrived(hy_r.at[2], tsem.at[8])
-        arrived(hy_r.at[1], tsem.at[9])
+        send(hy_s, hy_r.at[1], tsem.at[5], up)
+
+    def hy_end():
+        arrived(hy_r.at[2], tsem.at[4])
+        arrived(hy_r.at[1], tsem.at[5])
         res[0] = hy[y] + hy_r[1] + hy_r[2]
 
     def multiply(k):
-        b, zk = k % 3, zof(k)
+        b, zk = k, zof(k)
         for q in range(NG // GG):
             for h in range(2):
                 v = jnp.concatenate([xg[q * GG + i, zk, h] for i in range(GG)], axis=1)
@@ -269,7 +330,7 @@
                 part[b, j] = r if q == 0 else part[b, j] + r
 
     def rows(k, x_, h):
-        return lambda e: part[k % 3, x_ % 2, x_ // 2, (h * NB[0] + e) * HR:(h * NB[0] + e + 1) * HR, :]
+        return lambda e: part[k, x_ % 2, x_ // 2, (h * NB[0] + e) * HR:(h * NB[0] + e + 1) * HR, :]
 
     def compute(k):
         multiply(k)
@@ -294,10 +355,10 @@
                 arrived(xb_r.at[k, i, h, span(n)], bsem.at[k * 4 + i * 2 + h])
             terms = [rows(k, X, h), decoder(xb_r.at[k, 0, h], n), decoder(xb_r.at[k, 1, h], n)]
             for i in range(2):
-                sign = off if i == 0 else -off
-                if sign in (0, 1, 2) or (sign == 3 and h == i):
-                    arrived(z_r.at[k, i, h, span(n)], zsem.at[(k * 2 + i) * 2 + h])
-                    terms.append(decoder(z_r.at[k, i, h], n))
+                if (k, i, h) in HOPS:
+                    m = HOPS[k, i, h]
+                    arrived(z_r.at[m, span(n)], zsem.at[m])
+                    terms.append(decoder(z_r.at[m], n))
             get = plus(*terms)
             if off == 0:
                 for e in range(n):
@@ -305,53 +366,26 @@
                 continue
             encode(z_s.at[k, h], scales, n, get)
             i = h if off == 4 else (0 if off > 0 else 1)
-            m = OFFS.index((3, -3)[i] if off == 4 else (off - 1 if off > 0 else off + 1))
-            send(z_s.at[k, h, span(n)], z_r.at[m, i, h, span(n)], zsem.at[(m * 2 + i) * 2 + h], (ahead, behind)[i])
+            m = HOPS[OFFS.index((3, -3)[i] if off == 4 else (off - 1 if off > 0 else off + 1)), i, h]
+            send(z_s.at[k, h, span(n)], z_r.at[m, span(n)], zsem.at[m], (ahead, behind)[i])
 
     def czrows(k, u):
-        return lambda i: part[k % 3, i // 2, u, (NX1 + i % 2) * HR:(NX1 + i % 2 + 1) * HR, :]
-
-    def czsum(k):
-        off = OFFS[k]
-        for u in range(2):
-            terms = [czrows(k, u)]
-            for i in range(2):
-                sign = off if i == 0 else -off
-                if sign in (0, 1, 2) or (sign == 3 and u == i):
-                    arrived(cz_r.at[k, i, u], csem.at[(k * 2 + i) * 2 + u])
-                    terms.append(decoder(cz_r.at[k, i, u], 4))
-            get = plus(*terms)
-            if off == 0:
-                for i in range(4):
-                    cr[u * 2 + i // 2, i % 2] = get(i)
-                continue
-            encode(cz_s.at[k, u], scales, 4, get)
-            i = u if off == 4 else (0 if off > 0 else 1)
-            m = OFFS.index((3, -3)[i] if off == 4 else (off - 1 if off > 0 else off + 1))
-            send(cz_s.at[k, u], cz_r.at[m, i, u], csem.at[(m * 2 + i) * 2 + u], (ahead, behind)[i])
-
-    def cxsend():
-        for i, x_, dev in ((0, xp, right), (1, xm, left)):
-            send(cr.at[x2, i], cxa_r.at[i], cxsem.at[i], dev)
-            send(cr.at[x_, 1 - i], cxb_r.at[i, 1 - i], cxsem.at[2 + i * 2 + 1 - i], dev)
-
-    def cxsum():
-        for i, x_, dev in ((0, xp, right), (1, xm, left)):
-            arrived(cxa_r.at[i], cxsem.at[i])
-            cx_s[i] = cr[x_, i] + cxa_r[i]
-            send(cx_s.at[i], cxb_r.at[i, i], cxsem.at[2 + i * 2 + i], dev)
-
-    def cxlast():
-        for i in range(2):
-            for e in range(2):
-                arrived(cxb_r.at[i, e], cxsem.at[2 + i * 2 + e])
-        for e in range(2):
-            res[1 + NX1 + e] = cr[X, e] + cxb_r[0, e] + cxb_r[1, e]
+        return lambda i: part[k, i // 2, u, (NX1 + i % 2) * HR:(NX1 + i % 2 + 1) * HR, :]
+
+    def czput(u, i, v):
+        cr[u * 2 + i // 2, i % 2] = v
+
+    def cxput(e, v):
+        res[1 + NX1 + e] = v
+
+    czsum = over_z(czrows, 4, cz_s, cz_r, csem, czput)
+    cx_begin, cx_middle, cx_end = over_x(cr, cxa_r, cx_s, cxb_r, cxsem)
 
     arrived(xh_p, tsem.at[1])
     arrived(dyh_p, tsem.at[0])
     hmultiply()
-    hstart()
+    gx_begin()
+    hz(0)
     arrived(rel.at[0], dsem.at[0])
     send(rel.at[0], dyslot(0, ym * 2 + c), dsem.at[8], up)
     arrived(rel.at[1], dsem.at[1])
@@ -359,20 +393,29 @@
     arrived(xg.at[g_pa], tsem.at[2])
     xsend(0)
     xsend(1)
+    hz(1)
+    hz(2)
     gd, gu, gf = ym * 2 + c, yp * 2 + c, y2 * 2 + c
-    for n, (g, j, s) in enumerate(((gd, 0, 2), (gu, 0, 4), (gd, 1, 3), (gu, 1, 5))):
-        arrived(dyslot(j, g), dsem.at[s])
-        send(dyslot(j, g), dyslot(j, g), dsem.at[10 + n], partner)
-    for n, (g, j, s) in enumerate(((gf, 0, 8), (gf, 1, 9))):
-        arrived(dyslot(j, g), dsem.at[s])
-        send(dyslot(j, g), dyslot(j, g), dsem.at[14 + n], partner)
-    hstep(3)
+
+    def relay(n, g, j, i):
+        arrived(dyslot(j, g), dsem.at[i])
+        send(dyslot(j, g), dyslot(j, g), dsem.at[n], partner)
+
+    relay(10, gd, 0, 2)
+    relay(11, gu, 0, 4)
+    gx_middle()
+    relay(12, gd, 1, 3)
+    relay(13, gu, 1, 5)
+    relay(14, gf, 0, 8)
+    relay(15, gf, 1, 9)
     xforward(0)
+    gx_end()
+    gz(0)
     pd, pu, pf = ym * 2 + 1 - c, yp * 2 + 1 - c, y2 * 2 + 1 - c
     for g, j, s in ((g_pa, 0, 6), (g_pa, 1, 7), (pd, 0, 10), (pu, 0, 11), (pd, 1, 12), (pu, 1, 13), (pf, 0, 14), (pf, 1, 15)):
         arrived(dyslot(j, g), dsem.at[s])
 
-    for k in range(NZ):
+    def chunk(k):
         if k + 2 < NZ:
             xsend(k + 2)
         if k + 1 < NZ:
@@ -381,31 +424,60 @@
         arrived(xg.at[y2 * 2 + c, zk], xsem.at[k * 6 + 4])
         arrived(xg.at[y2 * 2 + 1 - c, zk], xsem.at[k * 6 + 5])
         compute(k)
-        czsum(k)
-        if k == NZ - 1:
-            cxsend()
-        if k >= 1:
-            xsum(k - 1)
-        if k >= 2:
-            zsum(k - 2)
-        if k == 0:
-            hstep(2)
-        elif k == 2:
-            hstep(1)
-        elif k == 3:
-            hlast()
-        elif k == 4:
-            hx()
-        elif k == 5:
-            hxlast()
-        elif k == 6:
-            hyadd()
-    cxsum()
-    xsum(NZ - 1)
-    zsum(NZ - 2)
-    hylast()
-    cxlast()
-    zsum(NZ - 1)
+
+    chunk(0)
+    czsum(0)
+    hz(3)
+    hz(4)
+    chunk(1)
+    chunk(2)
+    xsum(0)
+    czsum(1)
+    czsum(2)
+    gz(1)
+    gz(2)
+    chunk(3)
+    xsum(1)
+    hz(5)
+    hz(6)
+    chunk(4)
+    xsum(2)
+    zsum(0)
+    czsum(3)
+    czsum(4)
+    gz(3)
+    gz(4)
+    chunk(5)
+    xsum(3)
+    hz(7)
+    hx_begin()
+    chunk(6)
+    xsum(4)
+    zsum(1)
+    zsum(2)
+    czsum(5)
+    czsum(6)
+    gz(5)
+    gz(6)
+    chunk(7)
+    xsum(5)
+    hx_middle()
+    xsum(6)
+    zsum(3)
+    zsum(4)
+    gz(7)
+    czsum(7)
+    cx_begin()
+    hx_end(hyput)
+    hy_begin()
+    xsum(7)
+    cx_middle()
+    zsum(5)
+    zsum(6)
+    hy_middle()
+    cx_end(cxput)
+    hy_end()
+    zsum(7)
     for e in range(NE):
         v = res[0] * flag(e == hot)
         if e < NC:
@@ -421,6 +493,7 @@
     bf16, f32, i16 = jnp.bfloat16, jnp.float32, jnp.int16
     vm = pl.BlockSpec(memory_space=pltpu.VMEM)
     sem = pltpu.SemaphoreType.DMA
+    nh = len(HOPS)
     return pl.pallas_call(
         kernel,
         out_shape=jax.ShapeDtypeStruct((NE, HR, FC), f32),
@@ -440,34 +513,40 @@
             pltpu.VMEM((2, NG * TOK, FC), bf16),
             pltpu.VMEM((2, TOK, FC), bf16),
             pltpu.VMEM((2 * NC * HR, GG * TOK), bf16),
-            pltpu.VMEM((3, 2, 2, NC * HR, FC), f32),
+            pltpu.VMEM((NZ, 2, 2, NC * HR, FC), f32),
             pltpu.VMEM((8, NZ, 2, HR, FC), f32),
             pltpu.VMEM((NZ, 2, MSG, FC), i16),
             pltpu.VMEM((NZ, 2, MSG, FC), i16),
             pltpu.VMEM((NZ, 2, 2, MSG, FC), i16),
             pltpu.VMEM((NZ, 2, 2, MSG, FC), i16),
             pltpu.VMEM((NZ, 2, MSG, FC), i16),
-            pltpu.VMEM((NZ, 2, 2, MSG, FC), i16),
-            pltpu.VMEM((NZ, 4, MSG, FC), i16),
-            pltpu.VMEM((NZ, 2, 4, MSG, FC), i16),
-            pltpu.VMEM((4, 4, HR, FC), f32),
-            pltpu.VMEM((2, MSG, FC), i16),
-            pltpu.VMEM((2, MSG, FC), i16),
-            pltpu.VMEM((2, MSG, FC), i16),
-            pltpu.VMEM((2, MSG, FC), i16),
+            pltpu.VMEM((nh, MSG, FC), i16),
+            pltpu.VMEM((NZ, 2, MSG, FC), i16),
+            pltpu.VMEM((nh, MSG, FC), i16),
+            pltpu.VMEM((4, 2, HR, FC), f32),
+            pltpu.VMEM((2, HR, FC), f32),
+            pltpu.VMEM((2, HR, FC), f32),
+            pltpu.VMEM((2, 2, HR, FC), f32),
+            pltpu.VMEM((NZ, 2, MSG, FC), i16),
+            pltpu.VMEM((nh, MSG, FC), i16),
+            pltpu.VMEM((4, 2, HR, FC), f32),
+            pltpu.VMEM((2, HR, FC), f32),
+            pltpu.VMEM((2, HR, FC), f32),
+            pltpu.VMEM((2, 2, HR, FC), f32),
+            pltpu.VMEM((4, MSG, FC), i16),
+            pltpu.VMEM((4, MSG, FC), i16),
+            pltpu.VMEM((2, 4, MSG, FC), i16),
+            pltpu.VMEM((2, 4, MSG, FC), i16),
+            pltpu.VMEM((2, NZ, HR, FC), f32),
+            pltpu.VMEM((NZ, 2, HR, FC), f32),
+            pltpu.VMEM((nh, HR, FC), f32),
             pltpu.VMEM((4, HR, FC), f32),
             pltpu.VMEM((HR, FC), f32),
             pltpu.VMEM((3, HR, FC), f32),
             pltpu.VMEM((16, FC), f32),
-            pltpu.VMEM((NZ, 2, MSG, FC), i16),
-            pltpu.VMEM((NZ, 2, 2, MSG, FC), i16),
-            pltpu.VMEM((4, 2, HR, FC), f32),
-            pltpu.VMEM((2, HR, FC), f32),
-            pltpu.VMEM((2, HR, FC), f32),
-            pltpu.VMEM((2, 2, HR, FC), f32),
             pltpu.VMEM((NE, HR, FC), f32),
-            sem((16, 2)), sem((48, 2)), sem((16, 2)), sem((32, 2)), sem((32, 2)), sem((64, 2)), sem((10, 2)),
-            sem((32, 2)), sem((6, 2)), sem((2,)),
+            sem((16, 2)), sem((48, 2)), sem((16, 2)), sem((32, 2)), sem((nh, 2)), sem((nh, 2)), sem((6, 2)),
+            sem((nh, 2)), sem((6, 2)), sem((12, 2)), sem((nh, 2)), sem((6, 2)), sem((2,)),
         ],
         compiler_params=pltpu.CompilerParams(
             collective_id=0, has_side_effects=True, vmem_limit_bytes=58 << 20),

time: 80.9 us -> 73.4 us (0.907)
  Pallas kernels: 78.7 us -> 71.5 us
    pallas_call x1, Pallas kernels: 78.7 us -> 71.5 us  [shards(): pl.pallas_call(kernel, out_shape=jax.ShapeDtypeStruct((NE, HR, FC), f32),...]
where the time goes in v5:
time: 73.4 us; the launch traced here: 73.2 us
  Pallas kernels  71.5 us (97%)
  local copies, waits for them, and re-layouts  1.67 us (2%)
    pallas_call x1, Pallas kernels, shards(): pl.pallas_call(kernel, out_shape=jax.ShapeDtypeStruct((NE, HR, FC), f32),...  71.5 us
    unnamed x1, local copies, waits for them, and re-layouts  1.67 us

profile of v5, /device:TPU:8, one launch (start us, length us, event | category | flops | bytes accessed | tf_op | source)
XLA Modules:
  0.0 73.2 jit_solution(3048908459522169346)
XLA Ops:
  0.0 71.5 %shard_map.37 = f32[8,32,256]{2,1,0:T(8,128)} custom-call(s32[8,256]{1,0:T(8,128)} %bitcast.1, s32[8,256]{1,0:T(8,128)} %bitcast.2, bf16[512,1024]{1,0:T(8,128)(2,1)} %x_any.1, bf16[512,2048]{1,0:T(8,128)(2,1)} %dy_any.1), custom_call_target="tpu_custom_call" | custom-call | tf_op jit(solution)/shard_map/pallas_call | solution.py:497
  71.5 1.7 %copy.5 = f32[8,32,256]{2,1,0:T(8,128)} copy(f32[8,32,256]{2,1,0:T(8,128)} %shard_map.37) | data formatting | bytes 524288

commit v6 on v5

--- a/solution.py
+++ b/solution.py
@@ -72,7 +72,7 @@
 def kernel(seg, segv, x_any, dy_any, out, x, dy, msk, xo_h, xo_c, xh_p, xg, dyh_o, dyh_p, dyc, dyg, rel, lhs, part, hp,
            xa_s, xa_r, xb_s, xb_r, z_s, z_r, cz_s, cz_r, cr, cxa_r, cx_s, cxb_r, hz_s, hz_r, hr, ha_r, hs_s, hb_r,
            ga_s, ga_r, gb_s, gb_r, hq, hq_s, hq_r, hy, hy_s, hy_r, scales, res,
-           dsem, xsem, asem, bsem, zsem, csem, cxsem, hsem, hxsem, gsem, qsem, tsem, lsem):
+           dsem, xsem, asem, bsem, zsem, csem, cxsem, hsem, hxsem, gsem, qsem, tsem, lsem, ssem):
     dp, ex = lax.axis_index("dp"), lax.axis_index("expert")
     z, xh, c = dp // 4, (dp // 2) % 2, dp % 2
     xl, y = ex // NY, ex % NY
@@ -121,12 +121,6 @@
             picked.append((low, owner))
         return picked
 
-    for g in range(NG):
-        for j, (_, owner) in enumerate(cold_blocks(g)):
-            for e in range(NC):
-                name = e + jnp.where(e >= hot, 1, 0)
-                lanes = slice((g % GG) * TOK + j * BLOCK, (g % GG) * TOK + (j + 1) * BLOCK)
-                msk[g // GG, e:e + 1, lanes] = jnp.full((1, BLOCK), flag(owner == name), jnp.float32)
     low = [flag(c_[0]) for c_ in cold_blocks(g_me)]
 
     def pick(ref, j, i, n, width):
@@ -135,18 +129,19 @@
         return (a * jnp.full((1, width), w, jnp.float32).astype(a.dtype)
                 + b * jnp.full((1, width), 1.0 - w, jnp.float32).astype(b.dtype))
 
-    load_dy.wait()
-    for i, dst in ((1, dyc), (0, dyh_o)):
+    def choose(i, dst):
         for j in range(2):
             dst[j * BLOCK:(j + 1) * BLOCK, :] = pick(dy, j, i, slice(0, 8 * FC), 8 * FC)
-    load_x.wait()
+
+    load_dy.wait()
+    choose(1, dyc)
     pl.semaphore_wait(barrier, 7)
 
     started = []
 
     def copy(src, dst, sem, dev):
         return pltpu.make_async_remote_copy(
-            src_ref=src, dst_ref=dst, send_sem=sem.at[0], recv_sem=sem.at[1],
+            src_ref=src, dst_ref=dst, send_sem=ssem.at[0], recv_sem=sem,
             device_id=dev, device_id_type=pl.DeviceIdType.MESH)
 
     def send(src, dst, sem, dev):
@@ -165,13 +160,15 @@
 
     send(dyc.at[:, cols(y2, 0)], rel.at[0], dsem.at[0], up)
     send(dyc.at[:, cols(y2, 1)], rel.at[1], dsem.at[1], down)
-    send(dyh_o, dyh_p, tsem.at[0], partner)
     for j in range(2):
         send(dyc.at[:, cols(yp, j)], dyslot(j, g_me), dsem.at[2 + j], up)
         send(dyc.at[:, cols(ym, j)], dyslot(j, g_me), dsem.at[4 + j], down)
         send(dyc.at[:, cols(y, j)], dyslot(j, g_me), dsem.at[6 + j], partner)
+    choose(0, dyh_o)
+    send(dyh_o, dyh_p, tsem.at[0], partner)
     for j in range(2):
         dyg[j, pl.ds(pl.multiple_of(g_me * TOK, TOK), TOK)] = dyc[:, cols(y, j)]
+    load_x.wait()
 
     def turn(n, _):
         for j in range(4):
@@ -386,6 +383,12 @@
     hmultiply()
     gx_begin()
     hz(0)
+    for g in range(NG):
+        for j, (_, owner) in enumerate(cold_blocks(g)):
+            for e in range(NC):
+                name = e + jnp.where(e >= hot, 1, 0)
+                lanes = slice((g % GG) * TOK + j * BLOCK, (g % GG) * TOK + (j + 1) * BLOCK)
+                msk[g // GG, e:e + 1, lanes] = jnp.full((1, BLOCK), flag(owner == name), jnp.float32)
     arrived(rel.at[0], dsem.at[0])
     send(rel.at[0], dyslot(0, ym * 2 + c), dsem.at[8], up)
     arrived(rel.at[1], dsem.at[1])
@@ -393,6 +396,7 @@
     arrived(xg.at[g_pa], tsem.at[2])
     xsend(0)
     xsend(1)
+    xsend(2)
     hz(1)
     hz(2)
     gd, gu, gf = ym * 2 + c, yp * 2 + c, y2 * 2 + c
@@ -416,56 +420,57 @@
         arrived(dyslot(j, g), dsem.at[s])
 
     def chunk(k):
-        if k + 2 < NZ:
-            xsend(k + 2)
-        if k + 1 < NZ:
-            xforward(k + 1)
         zk = zof(k)
         arrived(xg.at[y2 * 2 + c, zk], xsem.at[k * 6 + 4])
         arrived(xg.at[y2 * 2 + 1 - c, zk], xsem.at[k * 6 + 5])
         compute(k)
-
+        if k + 3 < NZ:
+            xsend(k + 3)
+        if k + 2 < NZ:
+            xforward(k + 2)
+
+    xforward(1)
     chunk(0)
     czsum(0)
     hz(3)
     hz(4)
     chunk(1)
+    gz(1)
+    gz(2)
     chunk(2)
     xsum(0)
     czsum(1)
     czsum(2)
-    gz(1)
-    gz(2)
+    hz(5)
+    hz(6)
     chunk(3)
     xsum(1)
-    hz(5)
-    hz(6)
+    gz(3)
+    gz(4)
     chunk(4)
     xsum(2)
     zsum(0)
     czsum(3)
     czsum(4)
-    gz(3)
-    gz(4)
+    hz(7)
+    hx_begin()
     chunk(5)
     xsum(3)
-    hz(7)
-    hx_begin()
+    gz(5)
+    gz(6)
     chunk(6)
     xsum(4)
     zsum(1)
     zsum(2)
+    hx_middle()
     czsum(5)
     czsum(6)
-    gz(5)
-    gz(6)
     chunk(7)
     xsum(5)
-    hx_middle()
     xsum(6)
+    gz(7)
     zsum(3)
     zsum(4)
-    gz(7)
     czsum(7)
     cx_begin()
     hx_end(hyput)
@@ -496,7 +501,7 @@
     nh = len(HOPS)
     return pl.pallas_call(
         kernel,
-        out_shape=jax.ShapeDtypeStruct((NE, HR, FC), f32),
+        out_shape=pltpu.VMEM((NE, HR, FC), f32),
         in_specs=[pl.BlockSpec(memory_space=pltpu.SMEM), vm] + [pl.BlockSpec(memory_space=pl.ANY)] * 2,
         out_specs=vm,
         scratch_shapes=[
@@ -545,8 +550,8 @@
             pltpu.VMEM((3, HR, FC), f32),
             pltpu.VMEM((16, FC), f32),
             pltpu.VMEM((NE, HR, FC), f32),
-            sem((16, 2)), sem((48, 2)), sem((16, 2)), sem((32, 2)), sem((nh, 2)), sem((nh, 2)), sem((6, 2)),
-            sem((nh, 2)), sem((6, 2)), sem((12, 2)), sem((nh, 2)), sem((6, 2)), sem((2,)),
+            sem((16,)), sem((48,)), sem((16,)), sem((32,)), sem((nh,)), sem((nh,)), sem((6,)),
+            sem((nh,)), sem((6,)), sem((12,)), sem((nh,)), sem((6,)), sem((2,)), sem((1,)),
         ],
         compiler_params=pltpu.CompilerParams(
             collective_id=0, has_side_effects=True, vmem_limit_bytes=58 << 20),

time: 73.4 us -> 67.9 us (0.925)
  Pallas kernels: 71.5 us -> 66.8 us
  local copies, waits for them, and re-layouts: 1.67 us -> 0.71 us
    pallas_call x1, Pallas kernels: 71.5 us -> 66.8 us  [shards(): pl.pallas_call(kernel, out_shape=pltpu.VMEM((NE, HR, FC), f32), in_specs=...]
    unnamed x1, local copies, waits for them, and re-layouts: 1.67 us -> 0.71 us
where the time goes in v6:
time: 67.9 us; the launch traced here: 67.5 us
  Pallas kernels  66.8 us (98%)
  local copies, waits for them, and re-layouts  0.71 us (1%)
    pallas_call x1, Pallas kernels, shards(): pl.pallas_call(kernel, out_shape=pltpu.VMEM((NE, HR, FC), f32), in_specs=...  66.8 us

profile of v6, /device:TPU:8, one launch (start us, length us, event | category | flops | bytes accessed | tf_op | source)
XLA Modules:
  0.0 67.5 jit_solution(14050619813270270706)
XLA Ops:
  0.0 66.8 %shard_map.37 = f32[8,32,256]{2,1,0:T(8,128)S(1)} custom-call(s32[8,256]{1,0:T(8,128)} %bitcast.1, s32[8,256]{1,0:T(8,128)} %bitcast.2, bf16[512,1024]{1,0:T(8,128)(2,1)} %x_any.1, bf16[512,2048]{1,0:T(8,128)(2,1)} %dy_any.1), custom_call_target="tpu_custom_call" | custom-call | tf_op jit(solution)/shard_map/pallas_call | solution.py:502
  66.8 0.7 %copy.5 = f32[8,32,256]{2,1,0:T(8,128)} copy(f32[8,32,256]{2,1,0:T(8,128)S(1)} %shard_map.37) | data formatting | bytes 524288

commit v7 on v6

--- a/solution.py
+++ b/solution.py
@@ -69,7 +69,7 @@
 HOPS = hops()
 
 
-def kernel(seg, segv, x_any, dy_any, out, x, dy, msk, xo_h, xo_c, xh_p, xg, dyh_o, dyh_p, dyc, dyg, rel, lhs, part, hp,
+def kernel(seg_any, x_any, dy_any, out, seg, segv, x, dy, msk, xo_h, xo_c, xh_p, xg, dyh_o, dyh_p, dyc, dyg, rel, lhs, part, hp,
            xa_s, xa_r, xb_s, xb_r, z_s, z_r, cz_s, cz_r, cr, cxa_r, cx_s, cxb_r, hz_s, hz_r, hr, ha_r, hs_s, hb_r,
            ga_s, ga_r, gb_s, gb_r, hq, hq_s, hq_r, hy, hy_s, hy_r, scales, res,
            dsem, xsem, asem, bsem, zsem, csem, cxsem, hsem, hxsem, gsem, qsem, tsem, lsem, ssem):
@@ -95,9 +95,15 @@
         pl.semaphore_signal(barrier, inc=1, device_id=other, device_id_type=pl.DeviceIdType.MESH)
     load_dy = pltpu.make_async_copy(dy_any, dy, lsem.at[0])
     load_x = pltpu.make_async_copy(x_any, x, lsem.at[1])
+    loads = [pltpu.make_async_copy(seg_any, ref, lsem.at[2 + i]) for i, ref in enumerate((seg, segv))]
+    for op in loads:
+        op.start()
     load_dy.start()
     load_x.start()
     scales[...] = jnp.zeros_like(scales)
+
+    for op in loads:
+        op.wait()
 
     twos = jnp.min(jnp.where(segv[...] == 2, 1.0, 0.0), axis=1, keepdims=True)
     index = lax.broadcasted_iota(jnp.int32, (NE, 1), 0)
@@ -163,7 +169,7 @@
     for j in range(2):
         send(dyc.at[:, cols(yp, j)], dyslot(j, g_me), dsem.at[2 + j], up)
         send(dyc.at[:, cols(ym, j)], dyslot(j, g_me), dsem.at[4 + j], down)
-        send(dyc.at[:, cols(y, j)], dyslot(j, g_me), dsem.at[6 + j], partner)
+        send(dyc.at[:, cols(y, j)], dyslot(j, g_me), dsem.at[6], partner)
     choose(0, dyh_o)
     send(dyh_o, dyh_p, tsem.at[0], partner)
     for j in range(2):
@@ -188,17 +194,18 @@
     def xsend(k):
         zk = zof(k)
         for i, (s, g) in enumerate(((xo_c.at[c, zk], g_me), (xg.at[g_pa, zk], g_pa))):
-            send(s, xg.at[g, zk], xsem.at[k * 6 + i], up)
-            send(s, xg.at[g, zk], xsem.at[k * 6 + 2 + i], down)
+            send(s, xg.at[g, zk], xsem.at[k * 3], up)
+            send(s, xg.at[g, zk], xsem.at[k * 3 + 1], down)
+
+    def both(yy, k):
+        return xg.at[pl.ds(yy * 2, 2), zof(k)]
 
     def xforward(k):
         zk = zof(k)
-        for i in range(2):
-            g_d, g_u = ym * 2 + (c if i == 0 else 1 - c), yp * 2 + (c if i == 0 else 1 - c)
-            arrived(xg.at[g_d, zk], xsem.at[k * 6 + i])
-            arrived(xg.at[g_u, zk], xsem.at[k * 6 + 2 + i])
-        send(xg.at[ym * 2 + c, zk], xg.at[ym * 2 + c, zk], xsem.at[k * 6 + 4], up)
-        send(xg.at[yp * 2 + 1 - c, zk], xg.at[yp * 2 + 1 - c, zk], xsem.at[k * 6 + 5], down)
+        arrived(both(ym, k), xsem.at[k * 3])
+        arrived(both(yp, k), xsem.at[k * 3 + 1])
+        send(xg.at[ym * 2 + c, zk], xg.at[ym * 2 + c, zk], xsem.at[k * 3 + 2], up)
+        send(xg.at[yp * 2 + 1 - c, zk], xg.at[yp * 2 + 1 - c, zk], xsem.at[k * 3 + 2], down)
 
     def hmultiply():
         left_ = jnp.concatenate([xo_h[c].reshape(NZ * 2 * HR, TOK), xh_p[...].reshape(NZ * 2 * HR, TOK)], axis=1)
@@ -236,18 +243,16 @@
         def begin():
             for i, x_, dev in way:
                 send(acc.at[x2, i], a_r.at[i], sem.at[i], dev)
-                send(acc.at[x_, 1 - i], b_r.at[i, 1 - i], sem.at[2 + i * 2 + 1 - i], dev)
+                send(acc.at[x_, 1 - i], b_r.at[i, 1 - i], sem.at[2], dev)
 
         def middle():
             for i, x_, dev in way:
                 arrived(a_r.at[i], sem.at[i])
                 s_[i] = acc[x_, i] + a_r[i]
-                send(s_.at[i], b_r.at[i, i], sem.at[2 + i * 2 + i], dev)
+                send(s_.at[i], b_r.at[i, i], sem.at[2], dev)
 
         def end(put):
-            for i in range(2):
-                for e in range(2):
-                    arrived(b_r.at[i, e], sem.at[2 + i * 2 + e])
+            arrived(b_r, sem.at[2])
             for e in range(2):
                 put(e, acc[X, e] + b_r[0, e] + b_r[1, e])
         return begin, middle, end
@@ -276,17 +281,16 @@
         for t, dev in ((0, right), (2, left), (1, right), (3, left)):
             gsend(ga_s.at[t], ga_r.at[t], gsem.at[t], dev, grows(x2, t))
         for i, t, x_, dev in ((0, 2, xp, right), (1, 0, xm, left), (0, 3, xp, right), (1, 1, xm, left)):
-            gsend(gb_s.at[i, t], gb_r.at[i, t], gsem.at[4 + i * 4 + t], dev, grows(x_, t))
+            gsend(gb_s.at[i, t], gb_r.at[i, t], gsem.at[4 + t], dev, grows(x_, t))
 
     def gx_middle():
         for i, t, x_, dev in ((0, 0, xp, right), (1, 2, xm, left), (0, 1, xp, right), (1, 3, xm, left)):
             arrived(ga_r.at[t], gsem.at[t])
-            gsend(gb_s.at[i, t], gb_r.at[i, t], gsem.at[4 + i * 4 + t], dev, plus(grows(x_, t), decoder(ga_r.at[t], 4)))
+            gsend(gb_s.at[i, t], gb_r.at[i, t], gsem.at[4 + t], dev, plus(grows(x_, t), decoder(ga_r.at[t], 4)))
 
     def gx_end():
         for t in range(4):
-            for i in range(2):
-                arrived(gb_r.at[i, t], gsem.at[4 + i * 4 + t])
+            arrived(gb_r.at[:, t], gsem.at[4 + t])
             get = plus(grows(X, t), decoder(gb_r.at[0, t], 4), decoder(gb_r.at[1, t], 4))
             for i in range(4):
                 hq[i % 2, 2 * t + i // 2] = get(i)
@@ -336,20 +340,19 @@
             send(xa_s.at[k, h, span(NB[h])], xa_r.at[k, h, span(NB[h])], asem.at[k * 2 + h], dev)
         for i, h, x_, dev in ((0, 1, xp, right), (1, 0, xm, left)):
             encode(xb_s.at[k, i, h], scales, NB[h], rows(k, x_, h))
-            send(xb_s.at[k, i, h, span(NB[h])], xb_r.at[k, i, h, span(NB[h])], bsem.at[k * 4 + i * 2 + h], dev)
+            send(xb_s.at[k, i, h, span(NB[h])], xb_r.at[k, i, h, span(NB[h])], bsem.at[k * 2 + h], dev)
 
     def xsum(k):
         for h, x_, dev in ((0, xp, right), (1, xm, left)):
             arrived(xa_r.at[k, h, span(NB[h])], asem.at[k * 2 + h])
             encode(xb_s.at[k, h, h], scales, NB[h], plus(rows(k, x_, h), decoder(xa_r.at[k, h], NB[h])))
-            send(xb_s.at[k, h, h, span(NB[h])], xb_r.at[k, h, h, span(NB[h])], bsem.at[k * 4 + h * 2 + h], dev)
+            send(xb_s.at[k, h, h, span(NB[h])], xb_r.at[k, h, h, span(NB[h])], bsem.at[k * 2 + h], dev)
 
     def zsum(k):
         off = OFFS[k]
         for h in range(2):
             n = NB[h]
-            for i in range(2):
-                arrived(xb_r.at[k, i, h, span(n)], bsem.at[k * 4 + i * 2 + h])
+            arrived(xb_r.at[k, :, h, span(n)], bsem.at[k * 2 + h])
             terms = [rows(k, X, h), decoder(xb_r.at[k, 0, h], n), decoder(xb_r.at[k, 1, h], n)]
             for i in range(2):
                 if (k, i, h) in HOPS:
@@ -389,99 +392,96 @@
                 name = e + jnp.where(e >= hot, 1, 0)
                 lanes = slice((g % GG) * TOK + j * BLOCK, (g % GG) * TOK + (j + 1) * BLOCK)
                 msk[g // GG, e:e + 1, lanes] = jnp.full((1, BLOCK), flag(owner == name), jnp.float32)
-    arrived(rel.at[0], dsem.at[0])
-    send(rel.at[0], dyslot(0, ym * 2 + c), dsem.at[8], up)
-    arrived(rel.at[1], dsem.at[1])
-    send(rel.at[1], dyslot(1, yp * 2 + c), dsem.at[9], down)
     arrived(xg.at[g_pa], tsem.at[2])
     xsend(0)
-    xsend(1)
-    xsend(2)
+    arrived(rel.at[0], dsem.at[0])
+    send(rel.at[0], dyslot(0, ym * 2 + c), dsem.at[7], up)
+    arrived(rel.at[1], dsem.at[1])
+    send(rel.at[1], dyslot(1, yp * 2 + c), dsem.at[8], down)
     hz(1)
     hz(2)
     gd, gu, gf = ym * 2 + c, yp * 2 + c, y2 * 2 + c
 
-    def relay(n, g, j, i):
+    def relay(g, j, i):
         arrived(dyslot(j, g), dsem.at[i])
-        send(dyslot(j, g), dyslot(j, g), dsem.at[n], partner)
-
-    relay(10, gd, 0, 2)
-    relay(11, gu, 0, 4)
+        send(dyslot(j, g), dyslot(j, g), dsem.at[6], partner)
+
+    relay(gd, 0, 2)
+    relay(gu, 0, 4)
     gx_middle()
-    relay(12, gd, 1, 3)
-    relay(13, gu, 1, 5)
-    relay(14, gf, 0, 8)
-    relay(15, gf, 1, 9)
+    relay(gd, 1, 3)
+    relay(gu, 1, 5)
     xforward(0)
+    xsend(1)
+    xsend(2)
+    relay(gf, 0, 7)
+    relay(gf, 1, 8)
+    hz(3)
+    hz(4)
+    arrived(dyg.at[0], dsem.at[6])
+
+    def chunk(k):
+        arrived(both(y2, k), xsem.at[k * 3 + 2])
+        compute(k)
+        if k < NZ - 2:
+            xforward(k + 2)
+        if k < NZ - 4:
+            xsend(k + 4)
+
+    xforward(1)
+    xsend(3)
+    chunk(0)
+    czsum(0)
     gx_end()
     gz(0)
-    pd, pu, pf = ym * 2 + 1 - c, yp * 2 + 1 - c, y2 * 2 + 1 - c
-    for g, j, s in ((g_pa, 0, 6), (g_pa, 1, 7), (pd, 0, 10), (pu, 0, 11), (pd, 1, 12), (pu, 1, 13), (pf, 0, 14), (pf, 1, 15)):
-        arrived(dyslot(j, g), dsem.at[s])
-
-    def chunk(k):
-        zk = zof(k)
-        arrived(xg.at[y2 * 2 + c, zk], xsem.at[k * 6 + 4])
-        arrived(xg.at[y2 * 2 + 1 - c, zk], xsem.at[k * 6 + 5])
-        compute(k)
-        if k + 3 < NZ:
-            xsend(k + 3)
-        if k + 2 < NZ:
-            xforward(k + 2)
-
-    xforward(1)
-    chunk(0)
-    czsum(0)
-    hz(3)
-    hz(4)
     chunk(1)
     gz(1)
     gz(2)
+    hz(5)
+    hz(6)
     chunk(2)
     xsum(0)
     czsum(1)
     czsum(2)
-    hz(5)
-    hz(6)
     chunk(3)
     xsum(1)
     gz(3)
     gz(4)
+    hz(7)
+    hx_begin()
     chunk(4)
     xsum(2)
     zsum(0)
     czsum(3)
     czsum(4)
-    hz(7)
-    hx_begin()
     chunk(5)
     xsum(3)
     gz(5)
     gz(6)
+    hx_middle()
     chunk(6)
     xsum(4)
     zsum(1)
     zsum(2)
-    hx_middle()
     czsum(5)
     czsum(6)
     chunk(7)
     xsum(5)
+    gz(7)
+    hx_end(hyput)
+    hy_begin()
     xsum(6)
-    gz(7)
     zsum(3)
     zsum(4)
     czsum(7)
     cx_begin()
-    hx_end(hyput)
-    hy_begin()
     xsum(7)
+    hy_middle()
+    zsum(5)
     cx_middle()
-    zsum(5)
     zsum(6)
-    hy_middle()
+    hy_end()
     cx_end(cxput)
-    hy_end()
     zsum(7)
     for e in range(NE):
         v = res[0] * flag(e == hot)
@@ -502,9 +502,11 @@
     return pl.pallas_call(
         kernel,
         out_shape=pltpu.VMEM((NE, HR, FC), f32),
-        in_specs=[pl.BlockSpec(memory_space=pltpu.SMEM), vm] + [pl.BlockSpec(memory_space=pl.ANY)] * 2,
+        in_specs=[pl.BlockSpec(memory_space=pl.ANY)] * 3,
         out_specs=vm,
         scratch_shapes=[
+            pltpu.SMEM((NE, seg_blocks.shape[0]), jnp.int32),
+            pltpu.VMEM((NE, seg_blocks.shape[0]), jnp.int32),
             pltpu.VMEM(x_rows.shape, bf16),
             pltpu.VMEM(dy_rows.shape, bf16),
             pltpu.VMEM((NG // GG, NE, GG * TOK), f32),
@@ -550,12 +552,12 @@
             pltpu.VMEM((3, HR, FC), f32),
             pltpu.VMEM((16, FC), f32),
             pltpu.VMEM((NE, HR, FC), f32),
-            sem((16,)), sem((48,)), sem((16,)), sem((32,)), sem((nh,)), sem((nh,)), sem((6,)),
-            sem((nh,)), sem((6,)), sem((12,)), sem((nh,)), sem((6,)), sem((2,)), sem((1,)),
+            sem((9,)), sem((24,)), sem((16,)), sem((16,)), sem((nh,)), sem((nh,)), sem((3,)),
+            sem((nh,)), sem((3,)), sem((8,)), sem((nh,)), sem((6,)), sem((4,)), sem((1,)),
         ],
         compiler_params=pltpu.CompilerParams(
             collective_id=0, has_side_effects=True, vmem_limit_bytes=58 << 20),
-    )(seg_blocks.T, seg_blocks.T, x_rows, dy_rows)
+    )(seg_blocks.T, x_rows, dy_rows)
 
 
 def solution(mesh):

time: 67.9 us -> 65 us (0.957)
  Pallas kernels: 66.8 us -> 63.4 us
    pallas_call x1, Pallas kernels: 66.8 us -> 63.4 us  [shards(): pl.pallas_call(kernel, out_shape=pltpu.VMEM((NE, HR, FC), f32), in_specs=...]
where the time goes in v7:
time: 65 us; the launch traced here: 64.1 us
  Pallas kernels  63.4 us (98%)
  local copies, waits for them, and re-layouts  0.71 us (1%)
    pallas_call x1, Pallas kernels, shards(): pl.pallas_call(kernel, out_shape=pltpu.VMEM((NE, HR, FC), f32), in_specs=...  63.4 us

profile of v7, /device:TPU:8, one launch (start us, length us, event | category | flops | bytes accessed | tf_op | source)
XLA Modules:
  0.0 64.1 jit_solution(13673875212066260737)
XLA Ops:
  0.0 63.4 %shard_map.37 = f32[8,32,256]{2,1,0:T(8,128)S(1)} custom-call(s32[8,256]{1,0:T(8,128)} %bitcast.1, bf16[512,1024]{1,0:T(8,128)(2,1)} %x_any.1, bf16[512,2048]{1,0:T(8,128)(2,1)} %dy_any.1), custom_call_target="tpu_custom_call" | custom-call | tf_op jit(solution)/shard_map/pallas_call | solution.py:502
  63.4 0.7 %copy.5 = f32[8,32,256]{2,1,0:T(8,128)} copy(f32[8,32,256]{2,1,0:T(8,128)S(1)} %shard_map.37) | data formatting | bytes 524288

commit v8 on v7

--- a/solution.py
+++ b/solution.py
@@ -11,6 +11,7 @@
 NE = 8
 NC = NE - 1
 NX1 = 5
+NZ1 = NC - NX1
 NB = (3, 2)
 TOK = 2 * BLOCK
 NY, NX, NZ = 4, 4, 8
@@ -59,10 +60,8 @@
     found = {}
     for k, off in enumerate(OFFS):
         for i in range(2):
-            for u in range(2):
-                sign = off if i == 0 else -off
-                if sign in (0, 1, 2) or (sign == 3 and u == i):
-                    found[k, i, u] = len(found)
+            if (off if i == 0 else -off) in (0, 1, 2, 3):
+                found[k, i] = len(found)
     return found
 
 
@@ -213,47 +212,60 @@
             r = jnp.concatenate([dyh_o[:, n * FC:(n + 1) * FC], dyh_p[:, n * FC:(n + 1) * FC]], axis=0)
             hp[n] = jnp.dot(left_, r, preferred_element_type=jnp.float32).reshape(NZ, 2, HR, FC)
 
-    def over_z(rows_of, n, s_, r_, sem, last):
+    def over_z(rows_of, ns, s_, r_, sem, last):
+        total = ns[0] + ns[1]
+
         def step(k):
             off = OFFS[k]
-            for u in range(2):
-                terms = [rows_of(k, u)]
-                for i in range(2):
-                    if (k, i, u) in HOPS:
-                        m = HOPS[k, i, u]
-                        arrived(r_.at[m], sem.at[m])
-                        terms.append(decoder(r_.at[m], n) if n > 1 else lambda e, m=m: r_[m])
-                get = plus(*terms)
-                if off == 0:
-                    for e in range(n):
-                        last(u, e, get(e))
-                    continue
-                i = u if off == 4 else (0 if off > 0 else 1)
-                m = HOPS[OFFS.index((3, -3)[i] if off == 4 else (off - 1 if off > 0 else off + 1)), i, u]
-                if n > 1:
-                    encode(s_.at[k, u], scales, n, get)
-                else:
-                    s_[k, u] = get(0)
-                send(s_.at[k, u], r_.at[m], sem.at[m], (ahead, behind)[i])
+            terms = [[rows_of(k, u)] for u in range(2)]
+            for i in range(2):
+                if (k, i) in HOPS:
+                    m = HOPS[k, i]
+                    if off in (3, -3):
+                        arrived(r_.at[m, span(ns[i])], sem.at[m])
+                        terms[i].append(decoder(r_.at[m], ns[i]))
+                    else:
+                        arrived(r_.at[m, span(total)], sem.at[m])
+                        d = decoder(r_.at[m], total)
+                        terms[0].append(d)
+                        terms[1].append(lambda e, d=d: d(ns[0] + e))
+            halves = [plus(*t) for t in terms]
+            if off == 0:
+                for u in range(2):
+                    for e in range(ns[u]):
+                        last(u, e, halves[u](e))
+            elif off == 4:
+                for u in range(2):
+                    m = HOPS[1 + u, u]
+                    src = s_.at[(k, NZ)[u]]
+                    encode(src, scales, ns[u], halves[u])
+                    send(src.at[span(ns[u])], r_.at[m, span(ns[u])], sem.at[m], (ahead, behind)[u])
+            else:
+                i = 0 if off > 0 else 1
+                m = HOPS[OFFS.index(off - 1 if off > 0 else off + 1), i]
+                encode(s_.at[k], scales, total, lambda e: halves[0](e) if e < ns[0] else halves[1](e - ns[0]))
+                send(s_.at[k, span(total)], r_.at[m, span(total)], sem.at[m], (ahead, behind)[i])
         return step
 
     def over_x(acc, a_r, s_, b_r, sem):
-        way = ((0, xp, right), (1, xm, left))
+        n = acc.shape[1]
+        cut = (n + 1) // 2
+        way = ((pl.ds(0, cut), pl.ds(cut, n - cut), xp, right), (pl.ds(cut, n - cut), pl.ds(0, cut), xm, left))
 
         def begin():
-            for i, x_, dev in way:
-                send(acc.at[x2, i], a_r.at[i], sem.at[i], dev)
-                send(acc.at[x_, 1 - i], b_r.at[i, 1 - i], sem.at[2], dev)
+            for i, (mine, rest, x_, dev) in enumerate(way):
+                send(acc.at[x2, mine], a_r.at[mine], sem.at[i], dev)
+                send(acc.at[x_, rest], b_r.at[i, rest], sem.at[2], dev)
 
         def middle():
-            for i, x_, dev in way:
-                arrived(a_r.at[i], sem.at[i])
-                s_[i] = acc[x_, i] + a_r[i]
-                send(s_.at[i], b_r.at[i, i], sem.at[2], dev)
+            for i, (mine, _, x_, dev) in enumerate(way):
+                arrived(a_r.at[mine], sem.at[i])
+                s_[mine] = acc[x_, mine] + a_r[mine]
+                send(s_.at[mine], b_r.at[i, mine], sem.at[2], dev)
 
         def end(put):
             arrived(b_r, sem.at[2])
-            for e in range(2):
+            for e in range(n):
                 put(e, acc[X, e] + b_r[0, e] + b_r[1, e])
         return begin, middle, end
 
@@ -267,7 +279,7 @@
     def hyput(e, v):
         hy[2 + e] = v
 
-    hz = over_z(hrows, 4, hz_s, hz_r, hsem, hput)
+    hz = over_z(hrows, (4, 4), hz_s, hz_r, hsem, hput)
     hx_begin, hx_middle, hx_end = over_x(hr, ha_r, hs_s, hb_r, hxsem)
 
     def grows(x_, t):
@@ -302,7 +314,7 @@
     def qput(u, e, v):
         hy[u] = v
 
-    gz = over_z(qrows, 1, hq_s, hq_r, qsem, qput)
+    gz = over_z(qrows, (1, 1), hq_s, hq_r, qsem, qput)
 
     def hy_begin():
         send(hy.at[y2], hy_r.at[0], tsem.at[3], up)
@@ -335,50 +347,37 @@
 
     def compute(k):
         multiply(k)
-        for h, dev in ((0, right), (1, left)):
-            encode(xa_s.at[k, h], scales, NB[h], rows(k, x2, h))
-            send(xa_s.at[k, h, span(NB[h])], xa_r.at[k, h, span(NB[h])], asem.at[k * 2 + h], dev)
-        for i, h, x_, dev in ((0, 1, xp, right), (1, 0, xm, left)):
-            encode(xb_s.at[k, i, h], scales, NB[h], rows(k, x_, h))
-            send(xb_s.at[k, i, h, span(NB[h])], xb_r.at[k, i, h, span(NB[h])], bsem.at[k * 2 + h], dev)
+        for i, x_, dev in ((0, xp, right), (1, xm, left)):
+            far, near = rows(k, x2, i), rows(k, x_, 1 - i)
+            encode(xa_s.at[k, i], scales, NX1, lambda e: far(e) if e < NB[i] else near(e - NB[i]))
+            send(xa_s.at[k, i, span(NX1)], xa_r.at[k, i, span(NX1)], asem.at[k * 2 + i], dev)
 
     def xsum(k):
         for h, x_, dev in ((0, xp, right), (1, xm, left)):
-            arrived(xa_r.at[k, h, span(NB[h])], asem.at[k * 2 + h])
-            encode(xb_s.at[k, h, h], scales, NB[h], plus(rows(k, x_, h), decoder(xa_r.at[k, h], NB[h])))
-            send(xb_s.at[k, h, h, span(NB[h])], xb_r.at[k, h, h, span(NB[h])], bsem.at[k * 2 + h], dev)
-
-    def zsum(k):
-        off = OFFS[k]
-        for h in range(2):
-            n = NB[h]
-            arrived(xb_r.at[k, :, h, span(n)], bsem.at[k * 2 + h])
-            terms = [rows(k, X, h), decoder(xb_r.at[k, 0, h], n), decoder(xb_r.at[k, 1, h], n)]
-            for i in range(2):
-                if (k, i, h) in HOPS:
-                    m = HOPS[k, i, h]
-                    arrived(z_r.at[m, span(n)], zsem.at[m])
-                    terms.append(decoder(z_r.at[m], n))
-            get = plus(*terms)
-            if off == 0:
-                for e in range(n):
-                    res[1 + h * NB[0] + e] = get(e)
-                continue
-            encode(z_s.at[k, h], scales, n, get)
-            i = h if off == 4 else (0 if off > 0 else 1)
-            m = HOPS[OFFS.index((3, -3)[i] if off == 4 else (off - 1 if off > 0 else off + 1)), i, h]
-            send(z_s.at[k, h, span(n)], z_r.at[m, span(n)], zsem.at[m], (ahead, behind)[i])
+            arrived(xa_r.at[k, h, span(NX1)], asem.at[k * 2 + h])
+            encode(xb_s.at[k, h], scales, NB[h], plus(rows(k, x_, h), decoder(xa_r.at[k, h], NX1)))
+            send(xb_s.at[k, h, span(NB[h])], xb_r.at[k, h, span(NB[h])], bsem.at[k * 2 + h], dev)
+
+    def xrows(k, h):
+        arrived(xb_r.at[k, h, span(NB[h])], bsem.at[k * 2 + h])
+        d = decoder(xa_r.at[k, 1 - h], NX1)
+        return plus(rows(k, X, h), decoder(xb_r.at[k, h], NB[h]), lambda e: d(NB[1 - h] + e))
+
+    def xput(h, e, v):
+        res[1 + h * NB[0] + e] = v
+
+    zsum = over_z(xrows, NB, z_s, z_r, zsem, xput)
 
     def czrows(k, u):
-        return lambda i: part[k, i // 2, u, (NX1 + i % 2) * HR:(NX1 + i % 2 + 1) * HR, :]
+        return lambda i: part[k, i // NZ1, u, (NX1 + i % NZ1) * HR:(NX1 + i % NZ1 + 1) * HR, :]
 
     def czput(u, i, v):
-        cr[u * 2 + i // 2, i % 2] = v
+        cr[u * 2 + i // NZ1, i % NZ1] = v
 
     def cxput(e, v):
         res[1 + NX1 + e] = v
 
-    czsum = over_z(czrows, 4, cz_s, cz_r, csem, czput)
+    czsum = over_z(czrows, (2 * NZ1, 2 * NZ1), cz_s, cz_r, csem, czput)
     cx_begin, cx_middle, cx_end = over_x(cr, cxa_r, cx_s, cxb_r, cxsem)
 
     arrived(xh_p, tsem.at[1])
@@ -435,22 +434,22 @@
     gx_end()
     gz(0)
     chunk(1)
-    gz(1)
-    gz(2)
     hz(5)
     hz(6)
     chunk(2)
+    gz(1)
+    gz(2)
     xsum(0)
     czsum(1)
     czsum(2)
     chunk(3)
     xsum(1)
+    chunk(4)
+    xsum(2)
+    hz(7)
+    hx_begin()
     gz(3)
     gz(4)
-    hz(7)
-    hx_begin()
-    chunk(4)
-    xsum(2)
     zsum(0)
     czsum(3)
     czsum(4)
@@ -468,20 +467,20 @@
     chunk(7)
     xsum(5)
     gz(7)
-    hx_end(hyput)
-    hy_begin()
     xsum(6)
     zsum(3)
     zsum(4)
     czsum(7)
     cx_begin()
+    hx_end(hyput)
+    hy_begin()
     xsum(7)
+    cx_middle()
+    zsum(5)
     hy_middle()
-    zsum(5)
-    cx_middle()
     zsum(6)
+    cx_end(cxput)
     hy_end()
-    cx_end(cxput)
     zsum(7)
     for e in range(NE):
         v = res[0] * flag(e == hot)
@@ -522,20 +521,20 @@
             pltpu.VMEM((2 * NC * HR, GG * TOK), bf16),
             pltpu.VMEM((NZ, 2, 2, NC * HR, FC), f32),
             pltpu.VMEM((8, NZ, 2, HR, FC), f32),
+            pltpu.VMEM((NZ, 2, NX1 * HR + 16, FC), i16),
+            pltpu.VMEM((NZ, 2, NX1 * HR + 16, FC), i16),
             pltpu.VMEM((NZ, 2, MSG, FC), i16),
             pltpu.VMEM((NZ, 2, MSG, FC), i16),
-            pltpu.VMEM((NZ, 2, 2, MSG, FC), i16),
-            pltpu.VMEM((NZ, 2, 2, MSG, FC), i16),
-            pltpu.VMEM((NZ, 2, MSG, FC), i16),
-            pltpu.VMEM((nh, MSG, FC), i16),
-            pltpu.VMEM((NZ, 2, MSG, FC), i16),
-            pltpu.VMEM((nh, MSG, FC), i16),
-            pltpu.VMEM((4, 2, HR, FC), f32),
-            pltpu.VMEM((2, HR, FC), f32),
-            pltpu.VMEM((2, HR, FC), f32),
-            pltpu.VMEM((2, 2, HR, FC), f32),
-            pltpu.VMEM((NZ, 2, MSG, FC), i16),
-            pltpu.VMEM((nh, MSG, FC), i16),
+            pltpu.VMEM((NZ + 1, 5 * HR + 16, FC), i16),
+            pltpu.VMEM((nh, 5 * HR + 16, FC), i16),
+            pltpu.VMEM((NZ + 1, 4 * NZ1 * HR + 16, FC), i16),
+            pltpu.VMEM((nh, 4 * NZ1 * HR + 16, FC), i16),
+            pltpu.VMEM((4, NZ1, HR, FC), f32),
+            pltpu.VMEM((NZ1, HR, FC), f32),
+            pltpu.VMEM((NZ1, HR, FC), f32),
+            pltpu.VMEM((2, NZ1, HR, FC), f32),
+            pltpu.VMEM((NZ + 1, 8 * HR + 16, FC), i16),
+            pltpu.VMEM((nh, 8 * HR + 16, FC), i16),
             pltpu.VMEM((4, 2, HR, FC), f32),
             pltpu.VMEM((2, HR, FC), f32),
             pltpu.VMEM((2, HR, FC), f32),
@@ -545,8 +544,8 @@
             pltpu.VMEM((2, 4, MSG, FC), i16),
             pltpu.VMEM((2, 4, MSG, FC), i16),
             pltpu.VMEM((2, NZ, HR, FC), f32),
-            pltpu.VMEM((NZ, 2, HR, FC), f32),
-            pltpu.VMEM((nh, HR, FC), f32),
+            pltpu.VMEM((NZ + 1, 2 * HR + 16, FC), i16),
+            pltpu.VMEM((nh, 2 * HR + 16, FC), i16),
             pltpu.VMEM((4, HR, FC), f32),
             pltpu.VMEM((HR, FC), f32),
             pltpu.VMEM((3, HR, FC), f32),

time: 65 us -> 64.5 us (level); the launches traced: 64.1 us -> 64.4 us
  no operation moved by 1% of the time
where the time goes in v8:
time: 64.5 us; the launch traced here: 64.4 us
  Pallas kernels  63.6 us (99%)
  local copies, waits for them, and re-layouts  0.71 us (1%)
    pallas_call x1, Pallas kernels, shards(): pl.pallas_call(kernel, out_shape=pltpu.VMEM((NE, HR, FC), f32), in_specs=...  63.6 us

profile of v8, /device:TPU:8, one launch (start us, length us, event | category | flops | bytes accessed | tf_op | source)
XLA Modules:
  0.0 64.4 jit_solution(1420573181701993789)
XLA Ops:
  0.0 63.6 %shard_map.37 = f32[8,32,256]{2,1,0:T(8,128)S(1)} custom-call(s32[8,256]{1,0:T(8,128)} %bitcast.1, bf16[512,1024]{1,0:T(8,128)(2,1)} %x_any.1, bf16[512,2048]{1,0:T(8,128)(2,1)} %dy_any.1), custom_call_target="tpu_custom_call" | custom-call | tf_op jit(solution)/shard_map/pallas_call | solution.py:501
  63.6 0.7 %copy.5 = f32[8,32,256]{2,1,0:T(8,128)} copy(f32[8,32,256]{2,1,0:T(8,128)S(1)} %shard_map.37) | data formatting | bytes 524288
